TPU v7x, 256 devices: a 4x2x16 block of a 4x16x16 slice. The times are simulated.
256 devices in a mesh: scan: 2 (over y), slab: 128 (over z, x, core).
Axes of the slice: x: 4, y: 2, z: 16, core: 2. Of those that a mesh axis runs over, the one named last changes fastest.
The devices are a block of a 4x16x16 slice.
Arguments:
- image: float32 [2, 128, 256, 128], P(None, 'slab', 'scan'), parts along dimension 2, may hold values from -6 to 6
- sensitivity: bfloat16 [12, 2, 128, 128, 128], P('scan', None, 'slab'), parts along dimension 0, may hold values from -1.5 to 1.5
- kernel: float32 [256, 256, 256], P(None, 'slab'), may hold values from 0.1 to 4
Outputs:
- normal_image: float32 [2, 128, 256, 128], P(None, 'slab', 'scan'), parts along dimension 2
There are 2 independent parts, one for each index of `scan`. A program takes and returns all parts, laid end to end along the dimension named above; an argument that names none is the same for every part. Nothing has to cross between parts.
All inputs are finite; a program needn't handle non-finite values.
Results may differ from a plain program's by a relative error of at most 0.0024.
Values may be sent and summed in bfloat16 or wider, within the bound.
No kernel may reach another device: no remote copies, remote signals or barrier semaphores. Data moves between devices by JAX's collectives and lax.ppermute only.
A program may use at most 64 MiB of HBM per device.

v0:
```python
import math

import jax
import jax.numpy as jnp
from jax import lax
from jax.sharding import PartitionSpec as P

NX = 128
NY = 128
NZ = 128
GX = 256
GY = 256
GZ = 256


smooth_weight = 0.1


def with_halo(cells, sides, width):
    for axis, dim in sides:
        count = lax.axis_size(axis)
        ends = count - 1
        head = lax.slice_in_dim(cells, 0, width, axis=dim)
        tail = lax.slice_in_dim(cells, cells.shape[dim] - width, cells.shape[dim], axis=dim)
        cells = jnp.concatenate(
            [
                lax.ppermute(tail, axis, [(i, (i + 1) % count) for i in range(ends)]),
                cells,
                lax.ppermute(head, axis, [((i + 1) % count, i) for i in range(ends)]),
            ],
            axis=dim,
        )
    return cells


def fourier_table(count_out, count_in, length, sign_value):
    row_index = lax.broadcasted_iota(jnp.int32, (count_out, count_in), 0)
    column_index = lax.broadcasted_iota(jnp.int32, (count_out, count_in), 1)
    phases = row_index * column_index % length
    angles = phases.astype(jnp.float32) * (2.0 * math.pi / length)
    factor = 1.0 / math.sqrt(length)
    real_part = jnp.cos(angles) * factor
    imaginary = sign_value * jnp.sin(angles) * factor
    stacked = jnp.stack([jnp.stack([real_part, -imaginary]), jnp.stack([imaginary, real_part])])
    return stacked.astype(jnp.bfloat16)


def apply_table(matrix, values, pattern):
    return jnp.einsum(pattern, matrix, values, preferred_element_type=jnp.float32)


def local(image, sensitivity, kernel):
    forward_first = fourier_table(GX, NX, GX, -1.0)
    forward_second = fourier_table(GY, NY, GY, -1.0)
    forward_third = fourier_table(GZ, NZ, GZ, -1.0)
    inverse_first = fourier_table(NX, GX, GX, 1.0)
    inverse_second = fourier_table(NY, GY, GY, 1.0)
    inverse_third = fourier_table(NZ, GZ, GZ, 1.0)
    coil_real = sensitivity[:, 0].astype(jnp.float32)
    coil_imaginary = sensitivity[:, 1].astype(jnp.float32)
    coil_images = jnp.stack(
        [
            coil_real * image[0] - coil_imaginary * image[1],
            coil_real * image[1] + coil_imaginary * image[0],
        ],
        axis=1,
    ).astype(jnp.bfloat16)
    along_second = apply_table(forward_second, coil_images, "pqkj,cqajb->cpakb").astype(
        jnp.bfloat16
    )
    along_third = apply_table(
        forward_third,
        lax.all_to_all(along_second, "slab", split_axis=3, concat_axis=2, tiled=True),
        "pqkj,cqabj->cpabk",
    ).astype(jnp.bfloat16)
    spectrum = apply_table(forward_first, along_third, "pqkj,cqjab->cpkab")
    filtered = (spectrum * kernel).astype(jnp.bfloat16)
    back_first = apply_table(inverse_first, filtered, "pqkj,cqjab->cpkab").astype(jnp.bfloat16)
    back_third = apply_table(inverse_third, back_first, "pqkj,cqabj->cpabk").astype(jnp.bfloat16)
    back_third = lax.all_to_all(back_third, "slab", split_axis=2, concat_axis=3, tiled=True)
    coil_results = apply_table(inverse_second, back_third, "pqkj,cqajb->cpakb")
    summed_real = jnp.sum(
        coil_real * coil_results[:, 0] + coil_imaginary * coil_results[:, 1], axis=0
    )
    summed_imaginary = jnp.sum(
        coil_real * coil_results[:, 1] - coil_imaginary * coil_results[:, 0], axis=0
    )
    padded = with_halo(image.astype(jnp.bfloat16), (("slab", 1),), 1).astype(image.dtype)
    beside = padded[:, 2:] + padded[:, :-2]
    local_pad = jnp.pad(image, ((0, 0), (0, 0), (1, 1), (1, 1)))
    beside = beside + local_pad[:, :, 2:, 1:-1] + local_pad[:, :, :-2, 1:-1]
    beside = beside + local_pad[:, :, 1:-1, 2:] + local_pad[:, :, 1:-1, :-2]
    penalty = 6.0 * image - beside
    return jnp.stack([summed_real, summed_imaginary]) + smooth_weight * penalty


def solution(mesh):
    return jax.shard_map(
        local,
        mesh=mesh,
        in_specs=(
            P(None, "slab", "scan", None),
            P("scan", None, "slab", None, None),
            P(None, "slab", None),
        ),
        out_specs=P(None, "slab", "scan", None),
        check_vma=False,
    )
```

profile of v0, /device:TPU:33, one launch (start us, length us, event | category | flops | bytes accessed | tf_op | source)
XLA Modules:
  0.0 139.0 jit_solution(14245791856360535516)
XLA Ops:
  0.0 0.5 negate_convert_fusion.1
  0.6 0.5 fusion.58
  1.1 1.1 fusion.66
  2.1 0.2 copy.65
  2.3 0.2 copy.66
  2.5 0.1 copy.22
  2.6 0.1 copy.24
  2.7 0.1 fusion.38
  2.9 0.4 fusion.15
  3.3 0.0 copy-start
  3.3 1.9 %copy.26 = bf16[6,2,1,256,128]{4,1,0,2,3:T(2,128)(2,1)} copy(bf16[6,2,1,256,128]{3,4,1,0,2:T(8,128)(2,1)S(1)} %fusion.15) | data formatting | bytes 1572864 | tf_op jit(solution)/shard_map/convert_element_type | solution.py:68
  5.2 31.0 %all-to-all-start = ((bf16[6,2,1,256,128]{4,1,0,2,3:T(2,128)(2,1)}), bf16[6,2,1,256,128]{4,1,0,2,3:T(2,128)(2,1)S(1)}, u32[]{:S(2)}, u32[]{:S(2)}) async-start(bf16[6,2,1,256,128]{4,1,0,2,3:T(2,128)(2,1)} %copy.26), calls=%async_computation | async-start | bytes 1572864 | tf_op jit(solution)/shard_map/all_to_all | solution.py:73
  36.2 1.0 copy.30
  37.2 0.5 fusion.59
  37.7 0.5 negate_convert_fusion
  38.3 38.4 %all-to-all-done = bf16[6,2,1,256,128]{4,1,0,2,3:T(2,128)(2,1)S(1)} async-done(((bf16[6,2,1,256,128]{4,1,0,2,3:T(2,128)(2,1)}), bf16[6,2,1,256,128]{4,1,0,2,3:T(2,128)(2,1)S(1)}, u32[]{:S(2)}, u32[]{:S(2)}) %all-to-all-start) | async-done | bytes 786464 | tf_op jit(solution)/shard_map/all_to_all | solution.py:73
  76.7 0.6 bitcast_convert_fusion.1
  77.3 4.1 %bitcast_convert_fusion = bf16[6,2,256,2,128]{4,2,3,1,0:T(8,128)(2,1)} fusion(f32[256,2,256]{0,2,1:T(8,128)} %copy.30, bf16[6,128,2,2,256]{4,1,3,2,0:T(8,128)(2,1)S(1)} %bitcast_convert_fusion.1, bf16[1,2,128,256]{3,2,1,0:T(8,128)(2,1)S(1)} %get-tuple-element.14, bf16[1,2,128,256]{3,2,1,0:T(8,128)(2,1)S(1)} %get-tuple-element.13, ...), kind=kOutput, calls=%fused_computation.4 | convolution fusion | flops 1615593472 | bytes 4194304 | tf_op jit(solution)/shard_map/pqkj,cqjab->cpkab/dot_general | solution.py:49
  81.4 2.0 %fusion.16 = bf16[6,2,128,2,128]{4,2,1,3,0:T(8,128)(2,1)S(1)} fusion(bf16[6,2,256,2,128]{4,2,3,1,0:T(8,128)(2,1)} %bitcast_convert_fusion, bf16[1,2,128,256]{3,2,1,0:T(8,128)(2,1)S(1)} %get-tuple-element.14, bf16[1,2,128,256]{3,2,1,0:T(8,128)(2,1)S(1)} %get-tuple-element.13), kind=kOutput, calls=%fused_computation.15 | convolution fusion | flops 403570688 | bytes 2621440 | tf_op jit(solution)/shard_map/pqkj,cqabj->cpabk/dot_general | solution.py:49
  83.5 1.7 %copy.32 = bf16[6,2,128,2,128]{4,1,3,0,2:T(2,128)(2,1)} copy(bf16[6,2,128,2,128]{4,2,1,3,0:T(8,128)(2,1)S(1)} %fusion.16) | data formatting | bytes 1572864 | tf_op jit(solution)/shard_map/convert_element_type | solution.py:79
  85.1 11.4 %all-to-all-start.1 = ((bf16[6,2,128,2,128]{4,1,3,0,2:T(2,128)(2,1)}), bf16[6,2,128,2,128]{4,1,3,0,2:T(2,128)(2,1)S(1)}, u32[]{:S(2)}, u32[]{:S(2)}) async-start(bf16[6,2,128,2,128]{4,1,3,0,2:T(2,128)(2,1)} %copy.32), calls=%async_computation.1 | async-start | bytes 1572864 | tf_op jit(solution)/shard_map/all_to_all | solution.py:80
  96.5 0.1 copy.36
  96.7 3.6 %collective-permute-start = (bf16[2,1,128,128]{2,3,1,0:T(8,128)(2,1)S(1)}, bf16[2,1,128,128]{2,3,1,0:T(8,128)(2,1)S(1)}, u32[]{:S(2)}, u32[]{:S(2)}) collective-permute-start(bf16[2,1,128,128]{2,3,1,0:T(8,128)(2,1)S(1)} %convert_element_type.154), channel_id=1, source_target_pairs={{0,1},{1,2},{2,3},{3,4},{4,5},{5,6},{6,7},{7,8},{8,9},{9,10},{10,1... | collective-permute-start | bytes 196616 | tf_op jit(solution)/shard_map/ppermute | solution.py:27
  100.2 2.3 %collective-permute-start.1 = (bf16[2,1,128,128]{2,3,1,0:T(8,128)(2,1)S(1)}, bf16[2,1,128,128]{2,3,1,0:T(8,128)(2,1)S(1)}, u32[]{:S(2)}, u32[]{:S(2)}) collective-permute-start(bf16[2,1,128,128]{2,3,1,0:T(8,128)(2,1)S(1)} %convert_element_type.154), channel_id=1, source_target_pairs={{1,0},{2,1},{3,2},{4,3},{5,4},{6,5},{7,6},{8,7},{9,8},{10,9},{11,1... | collective-permute-start | bytes 196616 | tf_op jit(solution)/shard_map/ppermute | solution.py:29
  102.5 34.5 %all-to-all-done.1 = bf16[6,2,128,2,128]{4,1,3,0,2:T(2,128)(2,1)S(1)} async-done(((bf16[6,2,128,2,128]{4,1,3,0,2:T(2,128)(2,1)}), bf16[6,2,128,2,128]{4,1,3,0,2:T(2,128)(2,1)S(1)}, u32[]{:S(2)}, u32[]{:S(2)}) %all-to-all-start.1) | async-done | bytes 786464 | tf_op jit(solution)/shard_map/all_to_all | solution.py:80
  137.0 0.5 copy.33
  137.5 0.4 convolution_bitcast_fusion
  138.0 0.1 fusion.25
  138.1 0.0 collective-permute-done
  138.1 0.0 collective-permute-done.1
  138.1 0.1 fusion.51
  138.3 0.8 copy.39
  (7 shorter events, 0.1 us)
Async XLA Ops:
  0.0 2.5 %copy-start.1 = (f32[2,1,128,128]{3,2,1,0:T(8,128)S(1)}, f32[2,1,128,128]{3,2,1,0:T(8,128)}, u32[]{:S(2)}) copy-start(f32[2,1,128,128]{3,2,1,0:T(8,128)} %param.3) | copy-start | bytes 393220
  3.3 32.9 %copy-start = (f32[256,2,256]{2,1,0:T(2,128)S(1)}, f32[256,2,256]{2,1,0:T(2,128)}, u32[]{:S(2)}) copy-start(f32[256,2,256]{2,1,0:T(2,128)} %param.5) | copy-start | bytes 1572868
  5.2 71.5 %all-to-all-start = ((bf16[6,2,1,256,128]{4,1,0,2,3:T(2,128)(2,1)}), bf16[6,2,1,256,128]{4,1,0,2,3:T(2,128)(2,1)S(1)}, u32[]{:S(2)}, u32[]{:S(2)}) async-start(bf16[6,2,1,256,128]{4,1,0,2,3:T(2,128)(2,1)} %copy.26), calls=%async_computation | async-start | bytes 1572864 | tf_op jit(solution)/shard_map/all_to_all | solution.py:73
  85.1 51.9 %all-to-all-start.1 = ((bf16[6,2,128,2,128]{4,1,3,0,2:T(2,128)(2,1)}), bf16[6,2,128,2,128]{4,1,3,0,2:T(2,128)(2,1)S(1)}, u32[]{:S(2)}, u32[]{:S(2)}) async-start(bf16[6,2,128,2,128]{4,1,3,0,2:T(2,128)(2,1)} %copy.32), calls=%async_computation.1 | async-start | bytes 1572864 | tf_op jit(solution)/shard_map/all_to_all | solution.py:80
  96.7 41.4 %collective-permute-start = (bf16[2,1,128,128]{2,3,1,0:T(8,128)(2,1)S(1)}, bf16[2,1,128,128]{2,3,1,0:T(8,128)(2,1)S(1)}, u32[]{:S(2)}, u32[]{:S(2)}) collective-permute-start(bf16[2,1,128,128]{2,3,1,0:T(8,128)(2,1)S(1)} %convert_element_type.154), channel_id=1, source_target_pairs={{0,1},{1,2},{2,3},{3,4},{4,5},{5,6},{6,7},{7,8},{8,9},{9,10},{10,1... | collective-permute-start | bytes 196616 | tf_op jit(solution)/shard_map/ppermute | solution.py:27
  100.2 37.9 %collective-permute-start.1 = (bf16[2,1,128,128]{2,3,1,0:T(8,128)(2,1)S(1)}, bf16[2,1,128,128]{2,3,1,0:T(8,128)(2,1)S(1)}, u32[]{:S(2)}, u32[]{:S(2)}) collective-permute-start(bf16[2,1,128,128]{2,3,1,0:T(8,128)(2,1)S(1)} %convert_element_type.154), channel_id=1, source_target_pairs={{1,0},{2,1},{3,2},{4,3},{5,4},{6,5},{7,6},{8,7},{9,8},{10,9},{11,1... | collective-permute-start | bytes 196616 | tf_op jit(solution)/shard_map/ppermute | solution.py:29
where the time goes:
time: 141 us; the launch traced here: 139 us
  waiting for transfers between devices  72.9 us (52%)
  starting transfers between devices  48.2 us (34%)
  matrix products  7.59 us (5%)
  local copies, waits for them, and re-layouts  7.55 us (5%)
  other arithmetic  2.58 us (2%)
    all_to_all x1, waiting for transfers between devices, local(): lax.all_to_all(along_second, 'slab', split_axis=3, concat_axis=2, tiled=T...  38.4 us
    all_to_all x1, waiting for transfers between devices, local(): lax.all_to_all(back_third, 'slab', split_axis=2, concat_axis=3, tiled=True)  34.5 us
    all_to_all x1, starting transfers between devices, local(): lax.all_to_all(along_second, 'slab', split_axis=3, concat_axis=2, tiled=T...  31 us
    all_to_all x1, starting transfers between devices, local(): lax.all_to_all(back_third, 'slab', split_axis=2, concat_axis=3, tiled=True)  11.4 us
    dot_general x5, matrix products, apply_table(): jnp.einsum(pattern, matrix, values, preferred_element_type=jnp.float32)  7.59 us
    ppermute x1, starting transfers between devices, with_halo(): lax.ppermute(tail, axis, [(i, (i + 1) % count) for i in range(ends)])  3.57 us
  transfers between devices with their start and end apart: 4, of which 2 were waited for; matrix products, arithmetic and copies ran while one was open for 2% of the time, Pallas kernels for 0%

commit v1 on v0

v1 whole, which is shorter than its diff:
```python
import functools
import math

import jax
import jax.numpy as jnp
import ml_dtypes
import numpy as np
from jax import lax
from jax.experimental import pallas as pl
from jax.experimental.pallas import tpu as pltpu
from jax.sharding import Mesh
from jax.sharding import PartitionSpec as P

smooth_weight = 0.1
LAG_NS = 20000
VMEM, SMEM = pltpu.VMEM, pltpu.SMEM


def factor(count_out, count_in, length, sign_value):
    phases = np.outer(np.arange(count_out), np.arange(count_in)) % length
    angles = phases * (2.0 * math.pi / length)
    scale = 1.0 / math.sqrt(length)
    return np.cos(angles) * scale, sign_value * np.sin(angles) * scale


def held(table):
    return table.astype(np.float32).astype(ml_dtypes.bfloat16)


def stacked(real, imaginary):
    return np.block([[real, -imaginary], [imaginary, real]])


def second_tables(size, length, pair):
    real, imaginary = factor(length, size, length, -1.0)
    forward = np.stack(
        [np.concatenate([real, -imaginary], 1), np.concatenate([imaginary, real], 1)], 1
    )
    back_real, back_imaginary = factor(size, length, length, 1.0)
    inverse = np.stack(
        [
            np.concatenate([back_real, back_imaginary], 0),
            np.concatenate([-back_imaginary, back_real], 0),
        ],
        2,
    )
    base = np.arange(length).reshape(-1, 2, pair)
    orders = [base[:, ::step].reshape(-1) for step in (1, -1)]
    return (
        held(np.stack([forward[order].reshape(2 * length, 2 * size) for order in orders])),
        held(np.stack([inverse[:, order].reshape(2 * size, 2 * length) for order in orders])),
    )


def product(a, b):
    return jnp.dot(a, b, preferred_element_type=jnp.float32)


def coil_image_kernel(core_ref, image_ref, sensitivity_ref, own_ref, other_ref):
    core = core_ref[0]
    coils = own_ref.shape[0]
    image_real, image_imaginary = image_ref[0, 0], image_ref[1, 0]
    rows = image_real.shape[0]
    for ref, first in ((other_ref, (1 - core) * coils), (own_ref, core * coils)):
        for coil in range(coils):
            real = sensitivity_ref[first + coil, 0, 0].astype(jnp.float32)
            imaginary = sensitivity_ref[first + coil, 1, 0].astype(jnp.float32)
            ref[coil, :rows] = (real * image_real - imaginary * image_imaginary).astype(ref.dtype)
            ref[coil, rows:] = (real * image_imaginary + imaginary * image_real).astype(ref.dtype)


def second_kernel(core_ref, table_ref, own_ref, other_ref, out_ref):
    core = core_ref[0]
    groups, _, coils, rows, width = out_ref.shape
    table = table_ref[core]
    for ref, slot in ((own_ref, core), (other_ref, 1 - core)):
        for coil in range(coils):
            out_ref[:, slot, coil] = (
                product(table, ref[coil]).reshape(groups, rows, width).astype(out_ref.dtype)
            )

    @pl.when(core == 1)
    def _():
        pl.delay(LAG_NS)


def middle_kernel(
    in_ref, own_ref, other_ref, third_ref, first_ref, back_first_ref, back_third_ref,
    out_ref, lines, spread, filtered, back,
):
    count, coils, rows, width = in_ref.shape
    grid = own_ref.shape[0]
    frequencies = rows // 2

    @pl.loop(0, coils)
    def _(coil):
        lines[...] = in_ref[:, coil].astype(jnp.float32).reshape(count * rows, width)
        for j in range(frequencies):
            both = jnp.concatenate(
                [lines[pl.ds(2 * j + part, count, stride=rows), :] for part in range(2)], axis=1
            ).astype(jnp.bfloat16)
            third = product(both, third_ref[...]).astype(jnp.bfloat16)
            spread[:count] = third[:, :grid]
            spread[count:] = third[:, grid:]
            points_ref = (own_ref, other_ref)[j // (frequencies // 2)]
            at = j % (frequencies // 2) * grid
            points = points_ref[:, at : at + grid]
            for part in range(2):
                spectrum = product(first_ref[part * grid : (part + 1) * grid], spread[...])
                filtered[part * grid : (part + 1) * grid] = (spectrum * points).astype(jnp.bfloat16)
            first = product(back_first_ref[...], filtered[...]).astype(jnp.bfloat16)
            back[:, :grid] = first[:count]
            back[:, grid:] = first[count:]
            result = product(back[...], back_third_ref[...])
            for part in range(2):
                lines[pl.ds(2 * j + part, count, stride=rows), :] = result[
                    :, part * width : (part + 1) * width
                ]
        out_ref[:, coil] = lines[...].reshape(count, rows, width).astype(out_ref.dtype)


def last_kernel(core_ref, in_ref, table_ref, sensitivity_ref, out_ref, *, own):
    core = core_ref[0]
    groups, _, coils, rows, width = in_ref.shape
    table = table_ref[core]
    slot = core if own else 1 - core
    first = core * coils if own else 0
    size = table.shape[0] // 2
    real_sum = imaginary_sum = 0.0
    for coil in range(coils):
        values = product(table, in_ref[:, slot, coil].reshape(groups * rows, width))
        real = sensitivity_ref[first + coil, 0, 0].astype(jnp.float32)
        imaginary = sensitivity_ref[first + coil, 1, 0].astype(jnp.float32)
        real_sum += real * values[:size] + imaginary * values[size:]
        imaginary_sum += real * values[size:] - imaginary * values[:size]
    out_ref[0, 0] = real_sum
    out_ref[1, 0] = imaginary_sum


def call(kernel, name, out, spaces, operands, scratch=(), flops=0, mib=8):
    return pl.pallas_call(
        kernel,
        name=name,
        out_shape=out,
        in_specs=[pl.BlockSpec(memory_space=space) for space in spaces],
        out_specs=jax.tree.map(lambda _: pl.BlockSpec(memory_space=VMEM), out),
        scratch_shapes=scratch,
        compiler_params=pltpu.CompilerParams(vmem_limit_bytes=mib * 2**20),
        cost_estimate=pl.CostEstimate(flops=flops, bytes_accessed=2**20, transcendentals=0),
    )(*operands)


def local(image, sensitivity, kernel, *, groups, size):
    bf16, f32 = jnp.bfloat16, jnp.float32
    coils, width = sensitivity.shape[0] // 2, image.shape[3]
    grid, pair = kernel.shape[0], kernel.shape[1]
    rows = 4 * pair
    core = lax.axis_index("core")
    where = core.astype(jnp.int32).reshape(1)
    swap = [(0, 1), (1, 0)]
    shape = jax.ShapeDtypeStruct

    forward_second, inverse_second = second_tables(size, grid, pair)
    forward = factor(grid, size, grid, -1.0)
    inverse = factor(size, grid, grid, 1.0)
    first_table, back_first_table = held(stacked(*forward)), held(stacked(*inverse))
    third_table, back_third_table = held(stacked(*forward).T), held(stacked(*inverse).T)

    own_coils, other_coils = call(
        coil_image_kernel, "coil_images",
        (shape((coils, 2 * size, width), bf16),) * 2,
        (SMEM, VMEM, VMEM), (where, image, sensitivity), flops=2**20,
    )
    partner_coils = lax.ppermute(other_coils, "core", swap)
    sent = lax.dynamic_slice_in_dim(sensitivity, (1 - core) * coils, coils, 0)
    partner_sensitivity = lax.ppermute(sent, "core", swap)
    partner_image = lax.ppermute(image, "core", swap)
    own_coils, partner_coils, own_points, partner_points = lax.optimization_barrier(
        (own_coils, partner_coils, kernel, lax.ppermute(kernel, "core", swap))
    )
    own_points = own_points.reshape(grid, pair * grid)
    partner_points = partner_points.reshape(grid, pair * grid)

    payload = call(
        second_kernel, "along_second",
        shape((groups, 2, coils, rows, width), bf16),
        (SMEM, VMEM, VMEM, VMEM), (where, forward_second, own_coils, partner_coils), flops=2**28,
    )
    received = lax.all_to_all(payload, "chip", split_axis=0, concat_axis=0, tiled=True)
    returned = call(
        middle_kernel, "middle",
        shape((size, coils, rows, width), bf16),
        (VMEM,) * 7,
        (received.reshape(size, coils, rows, width), own_points, partner_points,
         third_table, first_table, back_first_table, back_third_table),
        (pltpu.VMEM((size * rows, width), f32), pltpu.VMEM((2 * size, grid), bf16),
         pltpu.VMEM((2 * grid, grid), bf16), pltpu.VMEM((size, 2 * grid), bf16)),
        flops=2**31, mib=16,
    )
    returned = lax.all_to_all(
        returned.reshape(groups, 2, coils, rows, width), "chip", split_axis=0, concat_axis=0, tiled=True
    )
    sums = [
        call(
            functools.partial(last_kernel, own=own), "along_second_back",
            shape(image.shape, f32), (SMEM, VMEM, VMEM, VMEM),
            (where, returned, inverse_second, weights), flops=2**28,
        )
        for own, weights in ((False, partner_sensitivity), (True, sensitivity))
    ]
    partner_sum = lax.ppermute(sums[0], "core", swap)

    ends = 2 * groups - 1
    outer = lax.ppermute(
        image,
        ("chip", "core"),
        [(i, i + 1) for i in range(1, ends, 2)] + [(i, i - 1) for i in range(2, ends + 1, 2)],
    )
    beside = partner_image + outer
    padded = jnp.pad(image, ((0, 0), (0, 0), (1, 1), (1, 1)))
    beside = beside + padded[:, :, 2:, 1:-1] + padded[:, :, :-2, 1:-1]
    beside = beside + padded[:, :, 1:-1, 2:] + padded[:, :, 1:-1, :-2]
    return sums[1] + partner_sum + smooth_weight * (6.0 * image - beside)


def solution(mesh):
    scans, slabs = mesh.devices.shape
    chips = Mesh(mesh.devices.reshape(scans, slabs // 2, 2), (mesh.axis_names[0], "chip", "core"))
    slab = ("chip", "core")
    return jax.shard_map(
        functools.partial(local, groups=slabs // 2, size=slabs),
        mesh=chips,
        in_specs=(
            P(None, slab, mesh.axis_names[0], None),
            P(mesh.axis_names[0], None, slab, None, None),
            P(None, slab, None),
        ),
        out_specs=P(None, slab, mesh.axis_names[0], None),
        check_vma=False,
    )
```

time: 141 us -> 127 us (0.901)
  Pallas kernels: 0 us -> 31.4 us
  waiting for transfers between devices: 72.9 us -> 50.8 us
  starting transfers between devices: 48.2 us -> 40.5 us
  matrix products: 7.59 us -> 0 us
  local copies, waits for them, and re-layouts: 7.55 us -> 2.74 us
  other arithmetic: 2.58 us -> 0.8 us
    pallas_call x0 -> x5, Pallas kernels: none -> 31.4 us  [call(): pl.pallas_call(kernel, name=name, out_shape=out, in_specs=[pl.BlockSpec(m...]
    all_to_all x2, starting transfers between devices: 42.4 us -> 17.2 us  [the longest x1 9.9 us: local(): lax.all_to_all(payload, 'chip', split_axis=0, concat_axis=0, tiled=True)]
    all_to_all x2, waiting for transfers between devices: 72.9 us -> 48.5 us  [the longest x1 25.9 us: local(): lax.all_to_all(payload, 'chip', split_axis=0, concat_axis=0, tiled=True)]
    ppermute x2 -> x6, starting transfers between devices: 5.82 us -> 23.3 us  [the longest x1 20.4 us: local(): lax.ppermute(kernel, 'core', swap)]
    dot_general x5 -> x0, matrix products: 7.59 us -> none  [apply_table(): jnp.einsum(pattern, matrix, values, preferred_element_type=jnp.float32)]
    convert_element_type x2 -> x0, local copies, waits for them, and re-layouts: 3.56 us -> none  [the longest x1 1.88 us: local(): apply_table(forward_second, coil_images, 'pqkj,cqajb->cpakb')]
    ppermute x2 -> x6, waiting for transfers between devices: 0.01 us -> 2.35 us  [the longest x1 1.42 us: local(): partner_coils = lax.ppermute(other_coils, 'core', swap)]
    another operation x7 -> x0, other arithmetic: 2.29 us -> none
  transfers between devices with their start and end apart: 4 -> 8, of which waited for: 2 -> 4; matrix products, arithmetic and copies ran while one was open for 2% -> 0% of each run, Pallas kernels for 0% -> 1%
where the time goes in v1:
time: 127 us; the launch traced here: 126 us
  waiting for transfers between devices  50.8 us (40%)
  starting transfers between devices  40.5 us (32%)
  Pallas kernels  31.4 us (25%)
  local copies, waits for them, and re-layouts  2.74 us (2%)
    pallas_call x5, Pallas kernels, call(): pl.pallas_call(kernel, name=name, out_shape=out, in_specs=[pl.BlockSpec(m...  31.4 us
    all_to_all x1, waiting for transfers between devices, local(): lax.all_to_all(payload, 'chip', split_axis=0, concat_axis=0, tiled=True)  25.9 us
    all_to_all x1, waiting for transfers between devices, local(): lax.all_to_all(returned.reshape(groups, 2, coils, rows, width), 'chip', s...  22.6 us
    ppermute x1, starting transfers between devices, local(): lax.ppermute(kernel, 'core', swap)  20.4 us
    all_to_all x1, starting transfers between devices, local(): lax.all_to_all(payload, 'chip', split_axis=0, concat_axis=0, tiled=True)  9.9 us
    all_to_all x1, starting transfers between devices, local(): lax.all_to_all(returned.reshape(groups, 2, coils, rows, width), 'chip', s...  7.26 us
    unnamed x20, local copies, waits for them, and re-layouts  2.72 us
  transfers between devices with their start and end apart: 8, of which 4 were waited for; matrix products, arithmetic and copies ran while one was open for 0% of the time, Pallas kernels for 1%

profile of v1, /device:TPU:33, one launch (start us, length us, event | category | flops | bytes accessed | tf_op | source)
XLA Modules:
  0.0 126.4 jit_solution(16484455623037817064)
XLA Ops:
  0.0 20.4 %collective-permute-start.1 = (f32[256,2,256]{2,1,0:T(2,128)}, f32[256,2,256]{2,1,0:T(2,128)S(1)}, u32[]{:S(2)}, u32[]{:S(2)}) collective-permute-start(f32[256,2,256]{2,1,0:T(2,128)} %param.11), channel_id=1, source_target_pairs={{0,1},{1,0},{2,3},{3,2},{4,5},{5,4},{6,7},{7,6},{8,9},{9,8},{10,11... | collective-permute-start | bytes 1572872 | tf_op jit(solution)/shard_map/ppermute | solution.py:179
  20.4 1.0 copy-done
  21.4 0.9 copy-done.4
  22.3 0.1 coil_images.1
  22.5 0.1 collective-permute-start
  22.6 1.4 %collective-permute-done.other_ref = bf16[3,256,128]{2,1,0:T(8,128)(2,1)S(1)} collective-permute-done((bf16[3,256,128]{2,1,0:T(8,128)(2,1)S(1)}, bf16[3,256,128]{2,1,0:T(8,128)(2,1)S(1)}, u32[]{:S(2)}, u32[]{:S(2)}) %collective-permute-start) | collective-permute-done | bytes 196640 | tf_op jit(solution)/shard_map/ppermute | solution.py:174
  24.0 0.0 collective-permute-done.1
  24.0 0.0 copy-done.3
  24.0 21.5 %along_second.1 = bf16[64,2,3,8,128]{4,3,2,1,0:T(8,128)(2,1)} custom-call(s32[1]{0:T(128)} %bitcast.core_ref, bf16[2,512,256]{2,1,0:T(8,128)(2,1)S(1)} %copy-done.3, bf16[3,256,128]{2,1,0:T(8,128)(2,1)S(1)} %get-tuple-element.13.own_ref, bf16[3,256,128]{2,1,0:T(8,128)(2,1)S(1)} %collective-permute-done.other_ref), custom_call_target="tpu_custom_call" | custom-call | flops 268435456 | bytes 1048576 | tf_op jit(solution)/shard_map/along_second/pallas_call | solution.py:141
  45.5 9.9 %all-to-all-start = ((bf16[64,2,3,8,128]{4,3,2,1,0:T(8,128)(2,1)}), bf16[64,2,3,8,128]{4,3,2,1,0:T(8,128)(2,1)S(1)}, u32[]{:S(2)}, u32[]{:S(2)}) async-start(bf16[64,2,3,8,128]{4,3,2,1,0:T(8,128)(2,1)} %along_second.1), calls=%async_computation | async-start | bytes 1572864 | tf_op jit(solution)/shard_map/all_to_all | solution.py:189
  55.4 0.0 copy-done.8
  55.5 0.0 copy-start.6
  55.5 0.0 copy-start.7
  55.5 25.9 %all-to-all-done = bf16[64,2,3,8,128]{4,3,2,1,0:T(8,128)(2,1)S(1)} async-done(((bf16[64,2,3,8,128]{4,3,2,1,0:T(8,128)(2,1)}), bf16[64,2,3,8,128]{4,3,2,1,0:T(8,128)(2,1)S(1)}, u32[]{:S(2)}, u32[]{:S(2)}) %all-to-all-start) | async-done | bytes 786464 | tf_op jit(solution)/shard_map/all_to_all | solution.py:189
  81.4 0.0 copy-done.6
  81.4 0.0 copy-done.7
  81.4 9.1 %middle.1 = bf16[128,3,8,128]{3,2,1,0:T(8,128)(2,1)} custom-call(bf16[128,3,8,128]{3,2,1,0:T(8,128)(2,1)S(1)} %bitcast.7, f32[256,512]{1,0:T(8,128)S(1)} %bitcast.8, f32[256,512]{1,0:T(8,128)S(1)} %bitcast.9, bf16[256,512]{1,0:T(8,128)(2,1)S(1)} %copy-done.6, bf16[512,256]{1,0:T(8,128)(2,1)S(1)} %copy-done.7, bf16[256,512]{1,0:T(8,128)(2,1)S(1)} %copy-done.6, ...), custom_call_target="tpu_custom_call" | custom-call | flops 2147483648 | bytes 1048576 | tf_op jit(solution)/shard_map/middle/pallas_call | solution.py:141
  90.5 7.3 %all-to-all-start.1 = ((bf16[64,2,3,8,128]{4,3,2,1,0:T(8,128)(2,1)}), bf16[64,2,3,8,128]{4,3,2,1,0:T(8,128)(2,1)S(1)}, u32[]{:S(2)}, u32[]{:S(2)}) async-start(bf16[64,2,3,8,128]{4,3,2,1,0:T(8,128)(2,1)} %bitcast.2), calls=%async_computation.1 | async-start | bytes 1572864 | tf_op jit(solution)/shard_map/all_to_all | solution.py:200
  97.8 0.0 copy-start.5
  97.8 0.1 collective-permute-start.2
  98.0 0.7 copy-done.5
  98.7 0.0 collective-permute-start.4
  98.7 2.5 %collective-permute-start.5 = (f32[2,1,128,128]{3,2,1,0:T(8,128)S(1)}, f32[2,1,128,128]{3,2,1,0:T(8,128)S(1)}, u32[]{:S(2)}, u32[]{:S(2)}) collective-permute-start(f32[2,1,128,128]{3,2,1,0:T(8,128)S(1)} %copy-done.5), channel_id=1, source_target_pairs={{1,2},{3,4},{5,6},{7,8},{9,10},{11,12},{13,14},{15,16},{17,18},{19... | collective-permute-start | bytes 393224 | tf_op jit(solution)/shard_map/ppermute | solution.py:214
  101.2 0.0 collective-permute-done.2.sensitivity_ref
  101.2 22.6 %all-to-all-done.1.in_ref = bf16[64,2,3,8,128]{4,3,2,1,0:T(8,128)(2,1)S(1)} async-done(((bf16[64,2,3,8,128]{4,3,2,1,0:T(8,128)(2,1)}), bf16[64,2,3,8,128]{4,3,2,1,0:T(8,128)(2,1)S(1)}, u32[]{:S(2)}, u32[]{:S(2)}) %all-to-all-start.1) | async-done | bytes 786464 | tf_op jit(solution)/shard_map/all_to_all | solution.py:200
  123.8 0.4 along_second_back.3
  124.1 0.1 collective-permute-start.3
  124.3 0.4 along_second_back.2
  124.7 0.0 collective-permute-done.4
  124.7 0.0 collective-permute-done.5
  124.7 0.9 collective-permute-done.3
  125.6 0.8 fusion.6
  (11 shorter events, 0.1 us)
Async XLA Ops:
  0.0 24.0 %collective-permute-start.1 = (f32[256,2,256]{2,1,0:T(2,128)}, f32[256,2,256]{2,1,0:T(2,128)S(1)}, u32[]{:S(2)}, u32[]{:S(2)}) collective-permute-start(f32[256,2,256]{2,1,0:T(2,128)} %param.11), channel_id=1, source_target_pairs={{0,1},{1,0},{2,3},{3,2},{4,5},{5,4},{6,7},{7,6},{8,9},{9,8},{10,11... | collective-permute-start | bytes 1572872 | tf_op jit(solution)/shard_map/ppermute | solution.py:179
  20.4 1.0 copy-start
  21.4 0.9 copy-start.4
  22.3 1.7 %copy-start.3 = (bf16[2,512,256]{2,1,0:T(8,128)(2,1)S(1)}, bf16[2,512,256]{2,1,0:T(8,128)(2,1)}, u32[]{:S(2)}) copy-start(bf16[2,512,256]{2,1,0:T(8,128)(2,1)} %constant.26.clone.table_ref) | copy-start | bytes 1572868
  22.5 1.6 %collective-permute-start = (bf16[3,256,128]{2,1,0:T(8,128)(2,1)S(1)}, bf16[3,256,128]{2,1,0:T(8,128)(2,1)S(1)}, u32[]{:S(2)}, u32[]{:S(2)}) collective-permute-start(bf16[3,256,128]{2,1,0:T(8,128)(2,1)S(1)} %get-tuple-element.12), channel_id=1, source_target_pairs={{0,1},{1,0},{2,3},{3,2},{4,5},{5,4},{6,7},{7,6},{8,9},{9,8},{10,11... | collective-permute-start | bytes 589832 | tf_op jit(solution)/shard_map/ppermute | solution.py:174
  45.5 9.9 %copy-start.8 = (f32[256,2,256]{2,1,0:T(2,128)S(1)}, f32[256,2,256]{2,1,0:T(2,128)}, u32[]{:S(2)}) copy-start(f32[256,2,256]{2,1,0:T(2,128)} %param.11) | copy-start | bytes 1572868
  45.5 35.9 %all-to-all-start = ((bf16[64,2,3,8,128]{4,3,2,1,0:T(8,128)(2,1)}), bf16[64,2,3,8,128]{4,3,2,1,0:T(8,128)(2,1)S(1)}, u32[]{:S(2)}, u32[]{:S(2)}) async-start(bf16[64,2,3,8,128]{4,3,2,1,0:T(8,128)(2,1)} %along_second.1), calls=%async_computation | async-start | bytes 1572864 | tf_op jit(solution)/shard_map/all_to_all | solution.py:189
  55.5 26.0 %copy-start.6 = (bf16[256,512]{1,0:T(8,128)(2,1)S(1)}, bf16[256,512]{1,0:T(8,128)(2,1)}, u32[]{:S(2)}) copy-start(bf16[256,512]{1,0:T(8,128)(2,1)} %constant.27.clone.third_ref.back_first_ref) | copy-start | bytes 786436
  55.5 25.9 %copy-start.7 = (bf16[512,256]{1,0:T(8,128)(2,1)S(1)}, bf16[512,256]{1,0:T(8,128)(2,1)}, u32[]{:S(2)}) copy-start(bf16[512,256]{1,0:T(8,128)(2,1)} %constant.28.clone.first_ref.back_third_ref) | copy-start | bytes 786436
  90.5 7.3 %copy-start.1 = (bf16[6,2,1,128,128]{4,3,2,1,0:T(8,128)(2,1)S(1)}, bf16[6,2,1,128,128]{4,3,2,1,0:T(8,128)(2,1)}, u32[]{:S(2)}) copy-start(bf16[6,2,1,128,128]{4,3,2,1,0:T(8,128)(2,1)} %sensitivity_ref.3) | copy-start | bytes 1179652
  90.5 33.3 %copy-start.2 = (bf16[2,256,512]{2,1,0:T(8,128)(2,1)S(1)}, bf16[2,256,512]{2,1,0:T(8,128)(2,1)}, u32[]{:S(2)}) copy-start(bf16[2,256,512]{2,1,0:T(8,128)(2,1)} %constant.29.clone.table_ref) | copy-start | bytes 1572868
  90.5 33.3 %all-to-all-start.1 = ((bf16[64,2,3,8,128]{4,3,2,1,0:T(8,128)(2,1)}), bf16[64,2,3,8,128]{4,3,2,1,0:T(8,128)(2,1)S(1)}, u32[]{:S(2)}, u32[]{:S(2)}) async-start(bf16[64,2,3,8,128]{4,3,2,1,0:T(8,128)(2,1)} %bitcast.2), calls=%async_computation.1 | async-start | bytes 1572864 | tf_op jit(solution)/shard_map/all_to_all | solution.py:200
  97.8 0.9 copy-start.5
  97.8 3.3 %collective-permute-start.2 = (bf16[3,2,1,128,128]{4,3,2,1,0:T(8,128)(2,1)S(1)}, bf16[3,2,1,128,128]{4,3,2,1,0:T(8,128)(2,1)S(1)}, u32[]{:S(2)}, u32[]{:S(2)}) collective-permute-start(bf16[3,2,1,128,128]{4,3,2,1,0:T(8,128)(2,1)S(1)} %constant_dynamic-slice_fusion), channel_id=1, source_target_pairs={{0,1},{1,0},{2,3},{3,2},{4,5},{5,4},{6,7},{7,6},{8,9},{9,8},{10,11... | collective-permute-start | bytes 589832 | tf_op jit(solution)/shard_map/ppermute | solution.py:176
  98.7 26.0 %collective-permute-start.4 = (f32[2,1,128,128]{3,2,1,0:T(8,128)S(1)}, f32[2,1,128,128]{3,2,1,0:T(8,128)S(1)}, u32[]{:S(2)}, u32[]{:S(2)}) collective-permute-start(f32[2,1,128,128]{3,2,1,0:T(8,128)S(1)} %copy-done.5), channel_id=1, source_target_pairs={{0,1},{1,0},{2,3},{3,2},{4,5},{5,4},{6,7},{7,6},{8,9},{9,8},{10,11... | collective-permute-start | bytes 393224 | tf_op jit(solution)/shard_map/ppermute | solution.py:177
  98.7 26.0 %collective-permute-start.5 = (f32[2,1,128,128]{3,2,1,0:T(8,128)S(1)}, f32[2,1,128,128]{3,2,1,0:T(8,128)S(1)}, u32[]{:S(2)}, u32[]{:S(2)}) collective-permute-start(f32[2,1,128,128]{3,2,1,0:T(8,128)S(1)} %copy-done.5), channel_id=1, source_target_pairs={{1,2},{3,4},{5,6},{7,8},{9,10},{11,12},{13,14},{15,16},{17,18},{19... | collective-permute-start | bytes 393224 | tf_op jit(solution)/shard_map/ppermute | solution.py:214
  124.1 1.5 %collective-permute-start.3 = (f32[2,1,128,128]{3,2,1,0:T(8,128)S(1)}, f32[2,1,128,128]{3,2,1,0:T(8,128)S(1)}, u32[]{:S(2)}, u32[]{:S(2)}) collective-permute-start(f32[2,1,128,128]{3,2,1,0:T(8,128)S(1)} %along_second_back.3), channel_id=1, source_target_pairs={{0,1},{1,0},{2,3},{3,2},{4,5},{5,4},{6,7},{7,6},{8,9},{9,8},{10,11... | collective-permute-start | bytes 393224 | tf_op jit(solution)/shard_map/ppermute | solution.py:211

commit v2 on v1

v2 whole, which is shorter than its diff:
```python
import functools
import math

import jax
import jax.numpy as jnp
import ml_dtypes
import numpy as np
from jax import lax
from jax.experimental import pallas as pl
from jax.experimental.pallas import tpu as pltpu
from jax.sharding import Mesh
from jax.sharding import PartitionSpec as P

smooth_weight = 0.1
LAG_NS = 18000
VMEM, SMEM, HBM = pltpu.VMEM, pltpu.SMEM, pltpu.HBM


def factor(count_out, count_in, length, sign_value):
    phases = np.outer(np.arange(count_out), np.arange(count_in)) % length
    angles = phases * (2.0 * math.pi / length)
    scale = 1.0 / math.sqrt(length)
    return np.cos(angles) * scale, sign_value * np.sin(angles) * scale


def held(table):
    return table.astype(np.float32).astype(ml_dtypes.bfloat16)


def stacked(real, imaginary):
    return np.block([[real, -imaginary], [imaginary, real]])


def second_tables(size, length, pair):
    real, imaginary = factor(length, size, length, -1.0)
    forward = np.stack(
        [np.concatenate([real, -imaginary], 1), np.concatenate([imaginary, real], 1)], 1
    )
    back_real, back_imaginary = factor(size, length, length, 1.0)
    inverse = np.stack(
        [
            np.concatenate([back_real, back_imaginary], 0),
            np.concatenate([-back_imaginary, back_real], 0),
        ],
        2,
    )
    base = np.arange(length).reshape(-1, 2, pair)
    orders = [base[:, ::step].reshape(-1) for step in (1, -1)]
    return (
        held(np.stack([forward[order].reshape(2 * length, 2 * size) for order in orders])),
        held(np.stack([inverse[:, order].reshape(2 * size, 2 * length) for order in orders])),
    )


def product(a, b):
    return jnp.dot(a, b, preferred_element_type=jnp.float32)


def coil_image_kernel(
    core_ref, image_ref, sensitivity_ref, own_ref, other_ref, image, sensitivity, arrived
):
    core = core_ref[0]
    coils = own_ref.shape[0]
    parts = ((other_ref, (1 - core) * coils), (own_ref, core * coils))
    copies = [pltpu.make_async_copy(image_ref, image, arrived.at[0])]
    copies += [
        pltpu.make_async_copy(
            sensitivity_ref.at[pl.ds(first, coils)], sensitivity.at[i], arrived.at[1 + i]
        )
        for i, (_, first) in enumerate(parts)
    ]
    for copy in copies:
        copy.start()
    copies[0].wait()
    image_real, image_imaginary = image[0, 0], image[1, 0]
    rows = image_real.shape[0]
    for i, (ref, _) in enumerate(parts):
        copies[1 + i].wait()
        for coil in range(coils):
            real = sensitivity[i, coil, 0, 0].astype(jnp.float32)
            imaginary = sensitivity[i, coil, 1, 0].astype(jnp.float32)
            ref[coil, :rows] = (real * image_real - imaginary * image_imaginary).astype(ref.dtype)
            ref[coil, rows:] = (real * image_imaginary + imaginary * image_real).astype(ref.dtype)


def second_kernel(core_ref, table_ref, coils_ref, *refs, own):
    out_ref, built, left = refs[-3:]
    core = core_ref[0]
    coils, groups, rows, width = built.shape
    table = table_ref[core]
    copies = []
    for coil in range(coils):
        built[coil] = (
            product(table, coils_ref[coil]).reshape(groups, rows, width).astype(built.dtype)
        )
        slot = core if own else 1 - core
        copies.append(
            pltpu.make_async_copy(built.at[coil], out_ref.at[:, slot, coil], left.at[coil])
        )
        copies[-1].start()
    for copy in copies:
        copy.wait()
    if not own:

        @pl.when(core == 1)
        def _():
            pl.delay(LAG_NS)


def middle_kernel(
    in_ref, own_ref, other_ref, third_ref, first_ref, back_first_ref, back_third_ref,
    out_ref, lines, both, spread, filtered, back, built, left,
):
    count, coils, rows, width = in_ref.shape
    grid = own_ref.shape[0]
    frequencies = rows // 2
    part_of = [slice(j * count, (j + 1) * count) for j in range(frequencies)]

    def copy_out(coil):
        return pltpu.make_async_copy(built.at[coil], out_ref.at[:, coil], left.at[coil])

    @pl.loop(0, coils)
    def _(coil):
        lines[...] = in_ref[:, coil].astype(jnp.float32).reshape(count * rows, width)
        for j in range(frequencies):
            for part in range(2):
                both[part_of[j], part * width : (part + 1) * width] = lines[
                    pl.ds(2 * j + part, count, stride=rows), :
                ].astype(jnp.bfloat16)
        for j in range(frequencies):
            third = product(both[part_of[j]], third_ref[...]).astype(jnp.bfloat16)
            spread[j, :count] = third[:, :grid]
            spread[j, count:] = third[:, grid:]
        for j in range(frequencies):
            points_ref = (own_ref, other_ref)[j // (frequencies // 2)]
            at = j % (frequencies // 2) * grid
            for part in range(2):
                half = slice(part * grid, (part + 1) * grid)
                spectrum = product(first_ref[half], spread[j])
                filtered[j, half] = (spectrum * points_ref[:, at : at + grid]).astype(jnp.bfloat16)
        for j in range(frequencies):
            first = product(back_first_ref[...], filtered[j]).astype(jnp.bfloat16)
            back[part_of[j], :grid] = first[:count]
            back[part_of[j], grid:] = first[count:]
        for j in range(frequencies):
            result = product(back[part_of[j]], back_third_ref[...])
            for part in range(2):
                lines[pl.ds(2 * j + part, count, stride=rows), :] = result[
                    :, part * width : (part + 1) * width
                ]
        built[coil] = lines[...].reshape(count, rows, width).astype(built.dtype)
        copy_out(coil).start()

    for coil in range(coils):
        copy_out(coil).wait()


def last_kernel(core_ref, in_ref, table_ref, sensitivity_ref, *refs, own):
    out_ref = refs[-1]
    core = core_ref[0]
    groups, _, coils, rows, width = in_ref.shape
    table = table_ref[core]
    slot = core if own else 1 - core
    first = core * coils if own else 0
    size = table.shape[0] // 2
    real_sum = imaginary_sum = 0.0
    for coil in range(coils):
        values = product(table, in_ref[:, slot, coil].reshape(groups * rows, width))
        real = sensitivity_ref[first + coil, 0, 0].astype(jnp.float32)
        imaginary = sensitivity_ref[first + coil, 1, 0].astype(jnp.float32)
        real_sum += real * values[:size] + imaginary * values[size:]
        imaginary_sum += real * values[size:] - imaginary * values[:size]
    if own:
        real_sum += refs[0][0, 0]
        imaginary_sum += refs[0][1, 0]
    out_ref[0, 0] = real_sum
    out_ref[1, 0] = imaginary_sum


def call(kernel, name, out, spaces, operands, scratch=(), flops=0, mib=8, to=VMEM, aliases=None):
    return pl.pallas_call(
        kernel,
        name=name,
        out_shape=out,
        in_specs=[pl.BlockSpec(memory_space=space) for space in spaces],
        out_specs=jax.tree.map(lambda _: pl.BlockSpec(memory_space=to), out),
        scratch_shapes=scratch,
        input_output_aliases=aliases or {},
        compiler_params=pltpu.CompilerParams(vmem_limit_bytes=mib * 2**20),
        cost_estimate=pl.CostEstimate(flops=flops, bytes_accessed=2**20, transcendentals=0),
    )(*operands)


def local(image, sensitivity, kernel, *, groups):
    bf16, f32 = jnp.bfloat16, jnp.float32
    coils, width = sensitivity.shape[0] // 2, image.shape[3]
    size, rows_second = 2 * groups * image.shape[1], image.shape[2]
    grid, pair = kernel.shape[0], kernel.shape[1]
    grid_second, grid_third = 2 * groups * pair, kernel.shape[2]
    rows = 4 * pair
    core = lax.axis_index("core")
    where = core.astype(jnp.int32).reshape(1)
    swap = [(0, 1), (1, 0)]
    shape = jax.ShapeDtypeStruct
    copies = pltpu.SemaphoreType.DMA

    forward_second, inverse_second = second_tables(rows_second, grid_second, pair)
    first_table = held(stacked(*factor(grid, size, grid, -1.0)))
    back_first_table = held(stacked(*factor(size, grid, grid, 1.0)))
    third_table = held(stacked(*factor(grid_third, width, grid_third, -1.0)).T)
    back_third_table = held(stacked(*factor(width, grid_third, grid_third, 1.0)).T)

    partner_points = lax.ppermute(kernel, "core", swap)
    own_coils, other_coils = call(
        coil_image_kernel, "coil_images",
        (shape((coils, 2 * rows_second, width), bf16),) * 2,
        (SMEM, HBM, HBM), (where, image, sensitivity),
        (VMEM(image.shape, f32), VMEM((2, coils, *sensitivity.shape[1:]), bf16), copies((3,))),
        flops=2**20,
    )
    partner_coils = lax.ppermute(other_coils, "core", swap)
    payload = None
    for own, values in ((True, own_coils), (False, partner_coils)):
        if not own:
            values, own_points, partner_points = lax.optimization_barrier(
                (values, kernel, partner_points)
            )
        payload = call(
            functools.partial(second_kernel, own=own), "along_second",
            shape((groups, 2, coils, rows, width), bf16),
            (SMEM, VMEM, VMEM) + (HBM,) * (not own),
            (where, forward_second, values) + (payload,) * (not own),
            (VMEM((coils, groups, rows, width), bf16), copies((coils,))),
            flops=2**28, to=HBM, aliases=None if own else {3: 0},
        )
    own_points = own_points.reshape(grid, pair * grid_third)
    partner_points = partner_points.reshape(grid, pair * grid_third)
    received = lax.all_to_all(payload, "chip", split_axis=0, concat_axis=0, tiled=True)
    returned = call(
        middle_kernel, "middle",
        shape((size, coils, rows, width), bf16),
        (VMEM,) * 7,
        (received.reshape(size, coils, rows, width), own_points, partner_points,
         third_table, first_table, back_first_table, back_third_table),
        (VMEM((size * rows, width), f32), VMEM((2 * pair * size, 2 * width), bf16),
         VMEM((2 * pair, 2 * size, grid_third), bf16), VMEM((2 * pair, 2 * grid, grid_third), bf16),
         VMEM((2 * pair * size, 2 * grid_third), bf16), VMEM((coils, size, rows, width), bf16),
         copies((coils,))),
        flops=2**31, mib=16, to=HBM,
    )
    returned = lax.all_to_all(
        returned.reshape(groups, 2, coils, rows, width), "chip", split_axis=0, concat_axis=0, tiled=True
    )

    ends = 2 * groups - 1
    partner_sensitivity = lax.ppermute(
        lax.dynamic_slice_in_dim(sensitivity, (1 - core) * coils, coils, 0), "core", swap
    )
    beside = lax.ppermute(image, "core", swap) + lax.ppermute(
        image,
        ("chip", "core"),
        [(i, i + 1) for i in range(1, ends, 2)] + [(i, i - 1) for i in range(2, ends + 1, 2)],
    )
    padded = jnp.pad(image, ((0, 0), (0, 0), (1, 1), (1, 1)))
    beside = beside + padded[:, :, 2:, 1:-1] + padded[:, :, :-2, 1:-1]
    beside = beside + padded[:, :, 1:-1, 2:] + padded[:, :, 1:-1, :-2]
    penalty = smooth_weight * (6.0 * image - beside)

    sums = [
        call(
            functools.partial(last_kernel, own=own), "along_second_back",
            shape(image.shape, f32), (SMEM,) + (VMEM,) * len(operands),
            (where, *operands), flops=2**28,
        )
        for own, operands in (
            (False, (returned, inverse_second, partner_sensitivity)),
            (True, (returned, inverse_second, sensitivity, penalty)),
        )
    ]
    return sums[1] + lax.ppermute(sums[0], "core", swap)


def solution(mesh):
    scans, slabs = mesh.devices.shape
    chips = Mesh(mesh.devices.reshape(scans, slabs // 2, 2), (mesh.axis_names[0], "chip", "core"))
    slab = ("chip", "core")
    return jax.shard_map(
        functools.partial(local, groups=slabs // 2),
        mesh=chips,
        in_specs=(
            P(None, slab, mesh.axis_names[0], None),
            P(mesh.axis_names[0], None, slab, None, None),
            P(None, slab, None),
        ),
        out_specs=P(None, slab, mesh.axis_names[0], None),
        check_vma=False,
    )
```

time: 127 us -> 121 us (0.953)
  Pallas kernels: 31.4 us -> 26 us
    pallas_call x5 -> x6, Pallas kernels: 31.4 us -> 26 us  [call(): pl.pallas_call(kernel, name=name, out_shape=out, in_specs=[pl.BlockSpec(m...]
  transfers between devices with their start and end apart: 8 -> 8, of which waited for: 4 -> 4; matrix products, arithmetic and copies ran while one was open for 0% -> 0% of each run, Pallas kernels for 1% -> 2%
where the time goes in v2:
time: 121 us
  waiting for transfers between devices  50.7 us (42%)
  starting transfers between devices  40.5 us (33%)
  Pallas kernels  26 us (21%)
  local copies, waits for them, and re-layouts  2.8 us (2%)
    pallas_call x6, Pallas kernels, call(): pl.pallas_call(kernel, name=name, out_shape=out, in_specs=[pl.BlockSpec(m...  26 us
    all_to_all x1, waiting for transfers between devices, local(): lax.all_to_all(payload, 'chip', split_axis=0, concat_axis=0, tiled=True)  25.9 us
    all_to_all x1, waiting for transfers between devices, local(): lax.all_to_all(returned.reshape(groups, 2, coils, rows, width), 'chip', s...  23.8 us
    ppermute x1, starting transfers between devices, local(): partner_points = lax.ppermute(kernel, 'core', swap)  20.4 us
    all_to_all x1, starting transfers between devices, local(): lax.all_to_all(payload, 'chip', split_axis=0, concat_axis=0, tiled=True)  9.92 us
    all_to_all x1, starting transfers between devices, local(): lax.all_to_all(returned.reshape(groups, 2, coils, rows, width), 'chip', s...  7.29 us
    unnamed x20, local copies, waits for them, and re-layouts  2.78 us
    ppermute x1, starting transfers between devices, local(): lax.ppermute(image, ('chip', 'core'), [(i, i + 1) for i in range(1, ends,...  2.46 us
  transfers between devices with their start and end apart: 8, of which 4 were waited for; matrix products, arithmetic and copies ran while one was open for 0% of the time, Pallas kernels for 2%

profile of v2, /device:TPU:33, one launch (start us, length us, event | category | flops | bytes accessed | tf_op | source)
XLA Modules:
  0.0 121.0 jit_solution(12607308199692057443)
XLA Ops:
  0.0 20.4 %collective-permute-start.1 = (f32[256,2,256]{2,1,0:T(2,128)}, f32[256,2,256]{2,1,0:T(2,128)S(1)}, u32[]{:S(2)}, u32[]{:S(2)}) collective-permute-start(f32[256,2,256]{2,1,0:T(2,128)} %param.11), channel_id=1, source_target_pairs={{0,1},{1,0},{2,3},{3,2},{4,5},{5,4},{6,7},{7,6},{8,9},{9,8},{10,11... | collective-permute-start | bytes 1572872 | tf_op jit(solution)/shard_map/ppermute | solution.py:213
  20.4 1.0 copy-done
  21.4 0.9 copy-done.4
  22.3 0.8 coil_images.1
  23.2 0.1 collective-permute-start
  23.3 0.1 copy-done.3
  23.4 1.1 along_second.2.refs_0_
  24.5 0.2 collective-permute-done.coils_ref
  24.7 19.2 %along_second.3 = bf16[64,2,3,8,128]{4,3,2,1,0:T(8,128)(2,1)} custom-call(s32[1]{0:T(128)} %bitcast.core_ref, bf16[2,512,256]{2,1,0:T(8,128)(2,1)S(1)} %copy-done.3, bf16[3,256,128]{2,1,0:T(8,128)(2,1)S(1)} %collective-permute-done.coils_ref, bf16[64,2,3,8,128]{4,3,2,1,0:T(8,128)(2,1)} %along_second.2.refs_0_), custom_call_target="tpu_custom_call", output_to_operand_aliasing={{}: (3, {})} | custom-call | flops 268435456 | bytes 1048576 | tf_op jit(solution)/shard_map/along_second/pallas_call | solution.py:181
  43.9 0.0 copy-start.8
  43.9 9.9 %all-to-all-start = ((bf16[64,2,3,8,128]{4,3,2,1,0:T(8,128)(2,1)}), bf16[64,2,3,8,128]{4,3,2,1,0:T(8,128)(2,1)S(1)}, u32[]{:S(2)}, u32[]{:S(2)}) async-start(bf16[64,2,3,8,128]{4,3,2,1,0:T(8,128)(2,1)} %along_second.3), calls=%async_computation | async-start | bytes 1572864 | tf_op jit(solution)/shard_map/all_to_all | solution.py:238
  53.9 0.0 copy-start.6
  53.9 0.0 copy-start.7
  53.9 25.9 %all-to-all-done = bf16[64,2,3,8,128]{4,3,2,1,0:T(8,128)(2,1)S(1)} async-done(((bf16[64,2,3,8,128]{4,3,2,1,0:T(8,128)(2,1)}), bf16[64,2,3,8,128]{4,3,2,1,0:T(8,128)(2,1)S(1)}, u32[]{:S(2)}, u32[]{:S(2)}) %all-to-all-start) | async-done | bytes 786464 | tf_op jit(solution)/shard_map/all_to_all | solution.py:238
  79.8 4.1 %middle.1 = bf16[128,3,8,128]{3,2,1,0:T(8,128)(2,1)} custom-call(bf16[128,3,8,128]{3,2,1,0:T(8,128)(2,1)S(1)} %bitcast.7, f32[256,512]{1,0:T(8,128)S(1)} %bitcast.8, f32[256,512]{1,0:T(8,128)S(1)} %bitcast.9, bf16[256,512]{1,0:T(8,128)(2,1)S(1)} %copy-done.6, bf16[512,256]{1,0:T(8,128)(2,1)S(1)} %copy-done.7, bf16[256,512]{1,0:T(8,128)(2,1)S(1)} %copy-done.6, ...), custom_call_target="tpu_custom_call" | custom-call | flops 2147483648 | bytes 1048576 | tf_op jit(solution)/shard_map/middle/pallas_call | solution.py:181
  84.0 0.0 copy-start.1
  84.0 0.0 copy-start.2
  84.0 7.3 %all-to-all-start.1 = ((bf16[64,2,3,8,128]{4,3,2,1,0:T(8,128)(2,1)}), bf16[64,2,3,8,128]{4,3,2,1,0:T(8,128)(2,1)S(1)}, u32[]{:S(2)}, u32[]{:S(2)}) async-start(bf16[64,2,3,8,128]{4,3,2,1,0:T(8,128)(2,1)} %bitcast.2), calls=%async_computation.1 | async-start | bytes 1572864 | tf_op jit(solution)/shard_map/all_to_all | solution.py:251
  91.3 0.0 copy-start.5
  91.3 0.1 collective-permute-start.4
  91.5 0.7 copy-done.5
  92.2 0.0 collective-permute-start.2
  92.2 2.5 %collective-permute-start.3 = (f32[2,1,128,128]{3,2,1,0:T(8,128)S(1)}, f32[2,1,128,128]{3,2,1,0:T(8,128)S(1)}, u32[]{:S(2)}, u32[]{:S(2)}) collective-permute-start(f32[2,1,128,128]{3,2,1,0:T(8,128)S(1)} %copy-done.5), channel_id=1, source_target_pairs={{1,2},{3,4},{5,6},{7,8},{9,10},{11,12},{13,14},{15,16},{17,18},{19... | collective-permute-start | bytes 393224 | tf_op jit(solution)/shard_map/ppermute | solution.py:259
  94.7 0.0 collective-permute-done.4.sensitivity_ref
  94.7 23.8 %all-to-all-done.1.in_ref = bf16[64,2,3,8,128]{4,3,2,1,0:T(8,128)(2,1)S(1)} async-done(((bf16[64,2,3,8,128]{4,3,2,1,0:T(8,128)(2,1)}), bf16[64,2,3,8,128]{4,3,2,1,0:T(8,128)(2,1)S(1)}, u32[]{:S(2)}, u32[]{:S(2)}) %all-to-all-start.1) | async-done | bytes 786464 | tf_op jit(solution)/shard_map/all_to_all | solution.py:251
  118.5 0.4 along_second_back.3
  118.9 0.1 collective-permute-start.5
  119.0 0.0 collective-permute-done.2
  119.1 0.1 fusion.5.refs_0_
  119.2 0.4 along_second_back.2
  119.6 0.8 collective-permute-done.5
  120.4 0.7 add.29
  (13 shorter events, 0.1 us)
Async XLA Ops:
  0.0 24.7 %collective-permute-start.1 = (f32[256,2,256]{2,1,0:T(2,128)}, f32[256,2,256]{2,1,0:T(2,128)S(1)}, u32[]{:S(2)}, u32[]{:S(2)}) collective-permute-start(f32[256,2,256]{2,1,0:T(2,128)} %param.11), channel_id=1, source_target_pairs={{0,1},{1,0},{2,3},{3,2},{4,5},{5,4},{6,7},{7,6},{8,9},{9,8},{10,11... | collective-permute-start | bytes 1572872 | tf_op jit(solution)/shard_map/ppermute | solution.py:213
  20.4 1.0 copy-start
  21.4 0.9 copy-start.4
  22.3 1.0 copy-start.3
  23.2 1.6 %collective-permute-start = (bf16[3,256,128]{2,1,0:T(8,128)(2,1)S(1)}, bf16[3,256,128]{2,1,0:T(8,128)(2,1)S(1)}, u32[]{:S(2)}, u32[]{:S(2)}) collective-permute-start(bf16[3,256,128]{2,1,0:T(8,128)(2,1)S(1)} %get-tuple-element.10), channel_id=1, source_target_pairs={{0,1},{1,0},{2,3},{3,2},{4,5},{5,4},{6,7},{7,6},{8,9},{9,8},{10,11... | collective-permute-start | bytes 589832 | tf_op jit(solution)/shard_map/ppermute | solution.py:221
  43.9 9.9 %copy-start.8 = (f32[256,2,256]{2,1,0:T(2,128)S(1)}, f32[256,2,256]{2,1,0:T(2,128)}, u32[]{:S(2)}) copy-start(f32[256,2,256]{2,1,0:T(2,128)} %param.11) | copy-start | bytes 1572868
  43.9 35.9 %all-to-all-start = ((bf16[64,2,3,8,128]{4,3,2,1,0:T(8,128)(2,1)}), bf16[64,2,3,8,128]{4,3,2,1,0:T(8,128)(2,1)S(1)}, u32[]{:S(2)}, u32[]{:S(2)}) async-start(bf16[64,2,3,8,128]{4,3,2,1,0:T(8,128)(2,1)} %along_second.3), calls=%async_computation | async-start | bytes 1572864 | tf_op jit(solution)/shard_map/all_to_all | solution.py:238
  53.9 25.9 %copy-start.6 = (bf16[256,512]{1,0:T(8,128)(2,1)S(1)}, bf16[256,512]{1,0:T(8,128)(2,1)}, u32[]{:S(2)}) copy-start(bf16[256,512]{1,0:T(8,128)(2,1)} %constant.27.clone.third_ref.back_first_ref) | copy-start | bytes 786436
  53.9 25.9 %copy-start.7 = (bf16[512,256]{1,0:T(8,128)(2,1)S(1)}, bf16[512,256]{1,0:T(8,128)(2,1)}, u32[]{:S(2)}) copy-start(bf16[512,256]{1,0:T(8,128)(2,1)} %constant.28.clone.first_ref.back_third_ref) | copy-start | bytes 786436
  84.0 7.3 %copy-start.1 = (bf16[6,2,1,128,128]{4,3,2,1,0:T(8,128)(2,1)S(1)}, bf16[6,2,1,128,128]{4,3,2,1,0:T(8,128)(2,1)}, u32[]{:S(2)}) copy-start(bf16[6,2,1,128,128]{4,3,2,1,0:T(8,128)(2,1)} %sensitivity_ref.3) | copy-start | bytes 1179652
  84.0 34.6 %copy-start.2 = (bf16[2,256,512]{2,1,0:T(8,128)(2,1)S(1)}, bf16[2,256,512]{2,1,0:T(8,128)(2,1)}, u32[]{:S(2)}) copy-start(bf16[2,256,512]{2,1,0:T(8,128)(2,1)} %constant.29.clone.table_ref) | copy-start | bytes 1572868
  84.0 34.5 %all-to-all-start.1 = ((bf16[64,2,3,8,128]{4,3,2,1,0:T(8,128)(2,1)}), bf16[64,2,3,8,128]{4,3,2,1,0:T(8,128)(2,1)S(1)}, u32[]{:S(2)}, u32[]{:S(2)}) async-start(bf16[64,2,3,8,128]{4,3,2,1,0:T(8,128)(2,1)} %bitcast.2), calls=%async_computation.1 | async-start | bytes 1572864 | tf_op jit(solution)/shard_map/all_to_all | solution.py:251
  91.3 0.9 copy-start.5
  91.3 3.3 %collective-permute-start.4 = (bf16[3,2,1,128,128]{4,3,2,1,0:T(8,128)(2,1)S(1)}, bf16[3,2,1,128,128]{4,3,2,1,0:T(8,128)(2,1)S(1)}, u32[]{:S(2)}, u32[]{:S(2)}) collective-permute-start(bf16[3,2,1,128,128]{4,3,2,1,0:T(8,128)(2,1)S(1)} %constant_dynamic-slice_fusion), channel_id=1, source_target_pairs={{0,1},{1,0},{2,3},{3,2},{4,5},{5,4},{6,7},{7,6},{8,9},{9,8},{10,11... | collective-permute-start | bytes 589832 | tf_op jit(solution)/shard_map/ppermute | solution.py:256
  92.2 26.8 %collective-permute-start.2 = (f32[2,1,128,128]{3,2,1,0:T(8,128)S(1)}, f32[2,1,128,128]{3,2,1,0:T(8,128)S(1)}, u32[]{:S(2)}, u32[]{:S(2)}) collective-permute-start(f32[2,1,128,128]{3,2,1,0:T(8,128)S(1)} %copy-done.5), channel_id=1, source_target_pairs={{0,1},{1,0},{2,3},{3,2},{4,5},{5,4},{6,7},{7,6},{8,9},{9,8},{10,11... | collective-permute-start | bytes 393224 | tf_op jit(solution)/shard_map/ppermute | solution.py:259
  92.2 26.9 %collective-permute-start.3 = (f32[2,1,128,128]{3,2,1,0:T(8,128)S(1)}, f32[2,1,128,128]{3,2,1,0:T(8,128)S(1)}, u32[]{:S(2)}, u32[]{:S(2)}) collective-permute-start(f32[2,1,128,128]{3,2,1,0:T(8,128)S(1)} %copy-done.5), channel_id=1, source_target_pairs={{1,2},{3,4},{5,6},{7,8},{9,10},{11,12},{13,14},{15,16},{17,18},{19... | collective-permute-start | bytes 393224 | tf_op jit(solution)/shard_map/ppermute | solution.py:259
  118.9 1.5 %collective-permute-start.5 = (f32[2,1,128,128]{3,2,1,0:T(8,128)S(1)}, f32[2,1,128,128]{3,2,1,0:T(8,128)S(1)}, u32[]{:S(2)}, u32[]{:S(2)}) collective-permute-start(f32[2,1,128,128]{3,2,1,0:T(8,128)S(1)} %along_second_back.3), channel_id=1, source_target_pairs={{0,1},{1,0},{2,3},{3,2},{4,5},{5,4},{6,7},{7,6},{8,9},{9,8},{10,11... | collective-permute-start | bytes 393224 | tf_op jit(solution)/shard_map/ppermute | solution.py:280

commit v3 on v2

--- a/solution.py
+++ b/solution.py
@@ -31,88 +31,75 @@
     return np.block([[real, -imaginary], [imaginary, real]])
 
 
-def second_tables(size, length, pair):
+def second_tables(size, length):
     real, imaginary = factor(length, size, length, -1.0)
     forward = np.stack(
         [np.concatenate([real, -imaginary], 1), np.concatenate([imaginary, real], 1)], 1
     )
-    back_real, back_imaginary = factor(size, length, length, 1.0)
+    real, imaginary = factor(size, length, length, 1.0)
     inverse = np.stack(
-        [
-            np.concatenate([back_real, back_imaginary], 0),
-            np.concatenate([-back_imaginary, back_real], 0),
-        ],
-        2,
-    )
-    base = np.arange(length).reshape(-1, 2, pair)
-    orders = [base[:, ::step].reshape(-1) for step in (1, -1)]
-    return (
-        held(np.stack([forward[order].reshape(2 * length, 2 * size) for order in orders])),
-        held(np.stack([inverse[:, order].reshape(2 * size, 2 * length) for order in orders])),
-    )
+        [np.concatenate([real, imaginary], 0), np.concatenate([-imaginary, real], 0)], 2
+    )
+    return held(forward.reshape(2 * length, -1)), held(inverse.reshape(-1, 2 * length))
 
 
 def product(a, b):
     return jnp.dot(a, b, preferred_element_type=jnp.float32)
 
 
-def coil_image_kernel(
-    core_ref, image_ref, sensitivity_ref, own_ref, other_ref, image, sensitivity, arrived
-):
+def coil_image_kernel(core_ref, image_ref, sensitivity_ref, own_ref, other_ref):
     core = core_ref[0]
     coils = own_ref.shape[0]
-    parts = ((other_ref, (1 - core) * coils), (own_ref, core * coils))
-    copies = [pltpu.make_async_copy(image_ref, image, arrived.at[0])]
-    copies += [
-        pltpu.make_async_copy(
-            sensitivity_ref.at[pl.ds(first, coils)], sensitivity.at[i], arrived.at[1 + i]
-        )
-        for i, (_, first) in enumerate(parts)
-    ]
-    for copy in copies:
-        copy.start()
-    copies[0].wait()
-    image_real, image_imaginary = image[0, 0], image[1, 0]
+    image_real, image_imaginary = image_ref[0, 0], image_ref[1, 0]
     rows = image_real.shape[0]
-    for i, (ref, _) in enumerate(parts):
-        copies[1 + i].wait()
+    for ref, first in ((other_ref, (1 - core) * coils), (own_ref, core * coils)):
         for coil in range(coils):
-            real = sensitivity[i, coil, 0, 0].astype(jnp.float32)
-            imaginary = sensitivity[i, coil, 1, 0].astype(jnp.float32)
+            real = sensitivity_ref[first + coil, 0, 0].astype(jnp.float32)
+            imaginary = sensitivity_ref[first + coil, 1, 0].astype(jnp.float32)
             ref[coil, :rows] = (real * image_real - imaginary * image_imaginary).astype(ref.dtype)
             ref[coil, rows:] = (real * image_imaginary + imaginary * image_real).astype(ref.dtype)
 
 
-def second_kernel(core_ref, table_ref, coils_ref, *refs, own):
-    out_ref, built, left = refs[-3:]
+def own_second_kernel(table_ref, coils_ref, built_ref):
+    table = table_ref[...]
+    coils, groups, rows, width = built_ref.shape
+    for coil in range(coils):
+        built_ref[coil] = (
+            product(table, coils_ref[coil]).reshape(groups, rows, width).astype(built_ref.dtype)
+        )
+
+
+def second_kernel(core_ref, table_ref, coils_ref, own_ref, out_ref, built, left):
     core = core_ref[0]
     coils, groups, rows, width = built.shape
-    table = table_ref[core]
-    copies = []
+    table = table_ref[...]
+
+    def copy_out(values, slot, coil, which):
+        return pltpu.make_async_copy(values, out_ref.at[:, slot, coil], left.at[which, coil])
+
+    for coil in range(coils):
+        copy_out(own_ref.at[coil], core, coil, 0).start()
     for coil in range(coils):
         built[coil] = (
             product(table, coils_ref[coil]).reshape(groups, rows, width).astype(built.dtype)
         )
-        slot = core if own else 1 - core
-        copies.append(
-            pltpu.make_async_copy(built.at[coil], out_ref.at[:, slot, coil], left.at[coil])
-        )
-        copies[-1].start()
-    for copy in copies:
-        copy.wait()
-    if not own:
-
-        @pl.when(core == 1)
-        def _():
-            pl.delay(LAG_NS)
+        copy_out(built.at[coil], 1 - core, coil, 1).start()
+    for coil in range(coils):
+        copy_out(own_ref.at[coil], core, coil, 0).wait()
+        copy_out(built.at[coil], 1 - core, coil, 1).wait()
+
+    @pl.when(core == 1)
+    def _():
+        pl.delay(LAG_NS)
 
 
 def middle_kernel(
-    in_ref, own_ref, other_ref, third_ref, first_ref, back_first_ref, back_third_ref,
+    core_ref, in_ref, points_ref, third_ref, first_ref, back_first_ref, back_third_ref,
     out_ref, lines, both, spread, filtered, back, built, left,
 ):
     count, coils, rows, width = in_ref.shape
-    grid = own_ref.shape[0]
+    grid = points_ref.shape[1]
+    core = core_ref[0]
     frequencies = rows // 2
     part_of = [slice(j * count, (j + 1) * count) for j in range(frequencies)]
 
@@ -132,12 +119,14 @@
             spread[j, :count] = third[:, :grid]
             spread[j, count:] = third[:, grid:]
         for j in range(frequencies):
-            points_ref = (own_ref, other_ref)[j // (frequencies // 2)]
+            place = core if j < frequencies // 2 else 1 - core
             at = j % (frequencies // 2) * grid
             for part in range(2):
                 half = slice(part * grid, (part + 1) * grid)
                 spectrum = product(first_ref[half], spread[j])
-                filtered[j, half] = (spectrum * points_ref[:, at : at + grid]).astype(jnp.bfloat16)
+                filtered[j, half] = (
+                    spectrum * points_ref[place, :, at : at + grid]
+                ).astype(jnp.bfloat16)
         for j in range(frequencies):
             first = product(back_first_ref[...], filtered[j]).astype(jnp.bfloat16)
             back[part_of[j], :grid] = first[:count]
@@ -159,7 +148,7 @@
     out_ref = refs[-1]
     core = core_ref[0]
     groups, _, coils, rows, width = in_ref.shape
-    table = table_ref[core]
+    table = table_ref[...]
     slot = core if own else 1 - core
     first = core * coils if own else 0
     size = table.shape[0] // 2
@@ -177,7 +166,7 @@
     out_ref[1, 0] = imaginary_sum
 
 
-def call(kernel, name, out, spaces, operands, scratch=(), flops=0, mib=8, to=VMEM, aliases=None):
+def call(kernel, name, out, spaces, operands, scratch=(), flops=0, mib=8, to=VMEM):
     return pl.pallas_call(
         kernel,
         name=name,
@@ -185,7 +174,6 @@
         in_specs=[pl.BlockSpec(memory_space=space) for space in spaces],
         out_specs=jax.tree.map(lambda _: pl.BlockSpec(memory_space=to), out),
         scratch_shapes=scratch,
-        input_output_aliases=aliases or {},
         compiler_params=pltpu.CompilerParams(vmem_limit_bytes=mib * 2**20),
         cost_estimate=pl.CostEstimate(flops=flops, bytes_accessed=2**20, transcendentals=0),
     )(*operands)
@@ -204,7 +192,7 @@
     shape = jax.ShapeDtypeStruct
     copies = pltpu.SemaphoreType.DMA
 
-    forward_second, inverse_second = second_tables(rows_second, grid_second, pair)
+    forward_second, inverse_second = second_tables(rows_second, grid_second)
     first_table = held(stacked(*factor(grid, size, grid, -1.0)))
     back_first_table = held(stacked(*factor(size, grid, grid, 1.0)))
     third_table = held(stacked(*factor(grid_third, width, grid_third, -1.0)).T)
@@ -214,33 +202,32 @@
     own_coils, other_coils = call(
         coil_image_kernel, "coil_images",
         (shape((coils, 2 * rows_second, width), bf16),) * 2,
-        (SMEM, HBM, HBM), (where, image, sensitivity),
-        (VMEM(image.shape, f32), VMEM((2, coils, *sensitivity.shape[1:]), bf16), copies((3,))),
+        (SMEM, VMEM, VMEM), (where, image, sensitivity),
         flops=2**20,
     )
     partner_coils = lax.ppermute(other_coils, "core", swap)
-    payload = None
-    for own, values in ((True, own_coils), (False, partner_coils)):
-        if not own:
-            values, own_points, partner_points = lax.optimization_barrier(
-                (values, kernel, partner_points)
-            )
-        payload = call(
-            functools.partial(second_kernel, own=own), "along_second",
-            shape((groups, 2, coils, rows, width), bf16),
-            (SMEM, VMEM, VMEM) + (HBM,) * (not own),
-            (where, forward_second, values) + (payload,) * (not own),
-            (VMEM((coils, groups, rows, width), bf16), copies((coils,))),
-            flops=2**28, to=HBM, aliases=None if own else {3: 0},
-        )
-    own_points = own_points.reshape(grid, pair * grid_third)
-    partner_points = partner_points.reshape(grid, pair * grid_third)
+    own_built = call(
+        own_second_kernel, "along_second",
+        shape((coils, groups, rows, width), bf16),
+        (VMEM, VMEM), (forward_second, own_coils), flops=2**28,
+    )
+    partner_coils, own_built, own_points, partner_points = lax.optimization_barrier(
+        (partner_coils, own_built, kernel, partner_points)
+    )
+    payload = call(
+        second_kernel, "along_second",
+        shape((groups, 2, coils, rows, width), bf16),
+        (SMEM, VMEM, VMEM, VMEM), (where, forward_second, partner_coils, own_built),
+        (VMEM((coils, groups, rows, width), bf16), copies((2, coils))),
+        flops=2**28, to=HBM,
+    )
+    points = jnp.stack([own_points, partner_points]).reshape(2, grid, pair * grid_third)
     received = lax.all_to_all(payload, "chip", split_axis=0, concat_axis=0, tiled=True)
     returned = call(
         middle_kernel, "middle",
         shape((size, coils, rows, width), bf16),
-        (VMEM,) * 7,
-        (received.reshape(size, coils, rows, width), own_points, partner_points,
+        (SMEM,) + (VMEM,) * 6,
+        (where, received.reshape(size, coils, rows, width), points,
          third_table, first_table, back_first_table, back_third_table),
         (VMEM((size * rows, width), f32), VMEM((2 * pair * size, 2 * width), bf16),
          VMEM((2 * pair, 2 * size, grid_third), bf16), VMEM((2 * pair, 2 * grid, grid_third), bf16),
@@ -253,14 +240,15 @@
     )
 
     ends = 2 * groups - 1
+    outer = lax.ppermute(
+        image.astype(bf16),
+        ("chip", "core"),
+        [(i, i + 1) for i in range(1, ends, 2)] + [(i, i - 1) for i in range(2, ends + 1, 2)],
+    )
     partner_sensitivity = lax.ppermute(
         lax.dynamic_slice_in_dim(sensitivity, (1 - core) * coils, coils, 0), "core", swap
     )
-    beside = lax.ppermute(image, "core", swap) + lax.ppermute(
-        image,
-        ("chip", "core"),
-        [(i, i + 1) for i in range(1, ends, 2)] + [(i, i - 1) for i in range(2, ends + 1, 2)],
-    )
+    beside = lax.ppermute(image, "core", swap) + outer.astype(f32)
     padded = jnp.pad(image, ((0, 0), (0, 0), (1, 1), (1, 1)))
     beside = beside + padded[:, :, 2:, 1:-1] + padded[:, :, :-2, 1:-1]
     beside = beside + padded[:, :, 1:-1, 2:] + padded[:, :, 1:-1, :-2]

time: 121 us -> 121 us (level)
  local copies, waits for them, and re-layouts: 2.8 us -> 4.76 us
  Pallas kernels: 26 us -> 24.5 us
  waiting for transfers between devices: 50.7 us -> 49.4 us
    pallas_call x6, Pallas kernels: 26 us -> 24.5 us  [call(): pl.pallas_call(kernel, name=name, out_shape=out, in_specs=[pl.BlockSpec(m...]
    all_to_all x1, waiting for transfers between devices: 25.9 us -> 24.5 us  [local(): lax.all_to_all(payload, 'chip', split_axis=0, concat_axis=0, tiled=True)]
    unnamed x20 -> x18, local copies, waits for them, and re-layouts: 2.78 us -> 3.9 us
  transfers between devices with their start and end apart: 8 -> 8, of which waited for: 4 -> 4; matrix products, arithmetic and copies ran while one was open for 0% -> 1% of each run, Pallas kernels for 2% -> 1%
where the time goes in v3:
time: 121 us; the launch traced here: 120 us
  waiting for transfers between devices  49.4 us (41%)
  starting transfers between devices  40.3 us (33%)
  Pallas kernels  24.5 us (20%)
  local copies, waits for them, and re-layouts  4.76 us (4%)
    pallas_call x6, Pallas kernels, call(): pl.pallas_call(kernel, name=name, out_shape=out, in_specs=[pl.BlockSpec(m...  24.5 us
    all_to_all x1, waiting for transfers between devices, local(): lax.all_to_all(payload, 'chip', split_axis=0, concat_axis=0, tiled=True)  24.5 us
    all_to_all x1, waiting for transfers between devices, local(): lax.all_to_all(returned.reshape(groups, 2, coils, rows, width), 'chip', s...  23.7 us
    ppermute x1, starting transfers between devices, local(): partner_points = lax.ppermute(kernel, 'core', swap)  20.4 us
    all_to_all x1, starting transfers between devices, local(): lax.all_to_all(payload, 'chip', split_axis=0, concat_axis=0, tiled=True)  9.78 us
    all_to_all x1, starting transfers between devices, local(): lax.all_to_all(returned.reshape(groups, 2, coils, rows, width), 'chip', s...  7.22 us
    unnamed x18, local copies, waits for them, and re-layouts  3.9 us
    ppermute x1, starting transfers between devices, local(): lax.ppermute(image.astype(bf16), ('chip', 'core'), [(i, i + 1) for i in r...  2.47 us
  transfers between devices with their start and end apart: 8, of which 4 were waited for; matrix products, arithmetic and copies ran while one was open for 1% of the time, Pallas kernels for 1%

profile of v3, /device:TPU:33, one launch (start us, length us, event | category | flops | bytes accessed | tf_op | source)
XLA Modules:
  0.0 120.1 jit_solution(17498283636557607290)
XLA Ops:
  0.0 20.4 %collective-permute-start.1 = (f32[256,2,256]{2,1,0:T(2,128)}, f32[256,2,256]{2,1,0:T(2,128)S(1)}, u32[]{:S(2)}, u32[]{:S(2)}) collective-permute-start(f32[256,2,256]{2,1,0:T(2,128)} %param.11), channel_id=1, source_target_pairs={{0,1},{1,0},{2,3},{3,2},{4,5},{5,4},{6,7},{7,6},{8,9},{9,8},{10,11... | collective-permute-start | bytes 1572872 | tf_op jit(solution)/shard_map/ppermute | solution.py:201
  20.4 1.0 copy-done
  21.4 0.9 copy-done.2
  22.3 0.1 coil_images.1
  22.5 0.1 collective-permute-start
  22.6 0.7 copy-done.5
  23.3 0.4 along_second.2.own_ref
  23.6 0.4 collective-permute-done.coils_ref
  24.0 19.2 %along_second.3 = bf16[64,2,3,8,128]{4,3,2,1,0:T(8,128)(2,1)} custom-call(s32[1]{0:T(128)} %bitcast.core_ref, bf16[512,256]{1,0:T(8,128)(2,1)S(1)} %copy-done.5, bf16[3,256,128]{2,1,0:T(8,128)(2,1)S(1)} %collective-permute-done.coils_ref, bf16[3,64,8,128]{3,2,1,0:T(8,128)(2,1)S(1)} %along_second.2.own_ref), custom_call_target="tpu_custom_call" | custom-call | flops 268435456 | bytes 1048576 | tf_op jit(solution)/shard_map/along_second/pallas_call | solution.py:170
  43.2 9.8 %all-to-all-start = ((bf16[64,2,3,8,128]{4,3,2,1,0:T(8,128)(2,1)}), bf16[64,2,3,8,128]{4,3,2,1,0:T(8,128)(2,1)S(1)}, u32[]{:S(2)}, u32[]{:S(2)}) async-start(bf16[64,2,3,8,128]{4,3,2,1,0:T(8,128)(2,1)} %along_second.3), calls=%async_computation | async-start | bytes 1572864 | tf_op jit(solution)/shard_map/all_to_all | solution.py:225
  53.0 0.0 copy-start.8
  53.0 0.4 stack.10
  53.5 0.6 copy-done.8
  54.1 0.4 stack.9
  54.5 0.0 copy-start.6
  54.5 0.0 copy-start.7
  54.5 0.1 pad_maximum_fusion.points_ref
  54.6 24.5 %all-to-all-done = bf16[64,2,3,8,128]{4,3,2,1,0:T(8,128)(2,1)S(1)} async-done(((bf16[64,2,3,8,128]{4,3,2,1,0:T(8,128)(2,1)}), bf16[64,2,3,8,128]{4,3,2,1,0:T(8,128)(2,1)S(1)}, u32[]{:S(2)}, u32[]{:S(2)}) %all-to-all-start) | async-done | bytes 786464 | tf_op jit(solution)/shard_map/all_to_all | solution.py:225
  79.1 4.1 %middle.1 = bf16[128,3,8,128]{3,2,1,0:T(8,128)(2,1)} custom-call(s32[1]{0:T(128)} %bitcast.core_ref, bf16[128,3,8,128]{3,2,1,0:T(8,128)(2,1)S(1)} %bitcast.3, f32[2,256,512]{2,1,0:T(8,128)S(1)} %pad_maximum_fusion.points_ref, bf16[256,512]{1,0:T(8,128)(2,1)S(1)} %copy-done.6, bf16[512,256]{1,0:T(8,128)(2,1)S(1)} %copy-done.7, ...), custom_call_target="tpu_custom_call" | custom-call | flops 2147483648 | bytes 1048576 | tf_op jit(solution)/shard_map/middle/pallas_call | solution.py:170
  83.3 7.2 %all-to-all-start.1 = ((bf16[64,2,3,8,128]{4,3,2,1,0:T(8,128)(2,1)}), bf16[64,2,3,8,128]{4,3,2,1,0:T(8,128)(2,1)S(1)}, u32[]{:S(2)}, u32[]{:S(2)}) async-start(bf16[64,2,3,8,128]{4,3,2,1,0:T(8,128)(2,1)} %bitcast.2), calls=%async_computation.1 | async-start | bytes 1572864 | tf_op jit(solution)/shard_map/all_to_all | solution.py:238
  90.5 0.0 copy-start.3
  90.5 0.0 copy-start.4
  90.5 0.1 collective-permute-start.4
  90.7 0.7 copy-done.3
  91.4 2.5 %collective-permute-start.3 = (bf16[2,1,128,128]{3,2,1,0:T(8,128)(2,1)S(1)}, bf16[2,1,128,128]{3,2,1,0:T(8,128)(2,1)S(1)}, u32[]{:S(2)}, u32[]{:S(2)}) collective-permute-start(bf16[2,1,128,128]{3,2,1,0:T(8,128)(2,1)S(1)} %convert_element_type.8), channel_id=1, source_target_pairs={{1,2},{3,4},{5,6},{7,8},{9,10},{11,12},{13,14},{15,16},{17,18},{19... | collective-permute-start | bytes 196616 | tf_op jit(solution)/shard_map/ppermute | solution.py:243
  93.9 23.7 %all-to-all-done.1.in_ref = bf16[64,2,3,8,128]{4,3,2,1,0:T(8,128)(2,1)S(1)} async-done(((bf16[64,2,3,8,128]{4,3,2,1,0:T(8,128)(2,1)}), bf16[64,2,3,8,128]{4,3,2,1,0:T(8,128)(2,1)S(1)}, u32[]{:S(2)}, u32[]{:S(2)}) %all-to-all-start.1) | async-done | bytes 786464 | tf_op jit(solution)/shard_map/all_to_all | solution.py:238
  117.6 0.4 along_second_back.3
  118.0 0.1 collective-permute-start.5
  118.1 0.1 fusion.5.refs_0_
  118.3 0.4 along_second_back.2
  118.7 0.8 collective-permute-done.5
  119.4 0.7 add.29
  (15 shorter events, 0.1 us)
Async XLA Ops:
  0.0 24.0 %collective-permute-start.1 = (f32[256,2,256]{2,1,0:T(2,128)}, f32[256,2,256]{2,1,0:T(2,128)S(1)}, u32[]{:S(2)}, u32[]{:S(2)}) collective-permute-start(f32[256,2,256]{2,1,0:T(2,128)} %param.11), channel_id=1, source_target_pairs={{0,1},{1,0},{2,3},{3,2},{4,5},{5,4},{6,7},{7,6},{8,9},{9,8},{10,11... | collective-permute-start | bytes 1572872 | tf_op jit(solution)/shard_map/ppermute | solution.py:201
  20.4 1.0 copy-start
  21.4 0.9 copy-start.2
  22.3 0.9 copy-start.5
  22.5 1.6 %collective-permute-start = (bf16[3,256,128]{2,1,0:T(8,128)(2,1)S(1)}, bf16[3,256,128]{2,1,0:T(8,128)(2,1)S(1)}, u32[]{:S(2)}, u32[]{:S(2)}) collective-permute-start(bf16[3,256,128]{2,1,0:T(8,128)(2,1)S(1)} %get-tuple-element.11), channel_id=1, source_target_pairs={{0,1},{1,0},{2,3},{3,2},{4,5},{5,4},{6,7},{7,6},{8,9},{9,8},{10,11... | collective-permute-start | bytes 589832 | tf_op jit(solution)/shard_map/ppermute | solution.py:208
  43.2 35.9 %all-to-all-start = ((bf16[64,2,3,8,128]{4,3,2,1,0:T(8,128)(2,1)}), bf16[64,2,3,8,128]{4,3,2,1,0:T(8,128)(2,1)S(1)}, u32[]{:S(2)}, u32[]{:S(2)}) async-start(bf16[64,2,3,8,128]{4,3,2,1,0:T(8,128)(2,1)} %along_second.3), calls=%async_computation | async-start | bytes 1572864 | tf_op jit(solution)/shard_map/all_to_all | solution.py:225
  53.0 1.0 copy-start.8
  54.5 24.6 %copy-start.6 = (bf16[256,512]{1,0:T(8,128)(2,1)S(1)}, bf16[256,512]{1,0:T(8,128)(2,1)}, u32[]{:S(2)}) copy-start(bf16[256,512]{1,0:T(8,128)(2,1)} %constant.27.clone.third_ref.back_first_ref) | copy-start | bytes 786436
  54.5 24.6 %copy-start.7 = (bf16[512,256]{1,0:T(8,128)(2,1)S(1)}, bf16[512,256]{1,0:T(8,128)(2,1)}, u32[]{:S(2)}) copy-start(bf16[512,256]{1,0:T(8,128)(2,1)} %constant.28.clone.first_ref.back_third_ref) | copy-start | bytes 786436
  83.2 7.2 %copy-start.1 = (bf16[6,2,1,128,128]{4,3,2,1,0:T(8,128)(2,1)S(1)}, bf16[6,2,1,128,128]{4,3,2,1,0:T(8,128)(2,1)}, u32[]{:S(2)}) copy-start(bf16[6,2,1,128,128]{4,3,2,1,0:T(8,128)(2,1)} %sensitivity_ref.3) | copy-start | bytes 1179652
  83.3 34.4 %all-to-all-start.1 = ((bf16[64,2,3,8,128]{4,3,2,1,0:T(8,128)(2,1)}), bf16[64,2,3,8,128]{4,3,2,1,0:T(8,128)(2,1)S(1)}, u32[]{:S(2)}, u32[]{:S(2)}) async-start(bf16[64,2,3,8,128]{4,3,2,1,0:T(8,128)(2,1)} %bitcast.2), calls=%async_computation.1 | async-start | bytes 1572864 | tf_op jit(solution)/shard_map/all_to_all | solution.py:238
  90.5 0.9 copy-start.3
  90.5 27.1 %copy-start.4 = (bf16[256,512]{1,0:T(8,128)(2,1)S(1)}, bf16[256,512]{1,0:T(8,128)(2,1)}, u32[]{:S(2)}) copy-start(bf16[256,512]{1,0:T(8,128)(2,1)} %constant.29.clone.table_ref) | copy-start | bytes 786436
  90.5 3.4 %collective-permute-start.4 = (bf16[3,2,1,128,128]{4,3,2,1,0:T(8,128)(2,1)S(1)}, bf16[3,2,1,128,128]{4,3,2,1,0:T(8,128)(2,1)S(1)}, u32[]{:S(2)}, u32[]{:S(2)}) collective-permute-start(bf16[3,2,1,128,128]{4,3,2,1,0:T(8,128)(2,1)S(1)} %constant_dynamic-slice_fusion), channel_id=1, source_target_pairs={{0,1},{1,0},{2,3},{3,2},{4,5},{5,4},{6,7},{7,6},{8,9},{9,8},{10,11... | collective-permute-start | bytes 589832 | tf_op jit(solution)/shard_map/ppermute | solution.py:248
  91.4 26.7 %collective-permute-start.2 = (f32[2,1,128,128]{3,2,1,0:T(8,128)S(1)}, f32[2,1,128,128]{3,2,1,0:T(8,128)S(1)}, u32[]{:S(2)}, u32[]{:S(2)}) collective-permute-start(f32[2,1,128,128]{3,2,1,0:T(8,128)S(1)} %copy-done.3), channel_id=1, source_target_pairs={{0,1},{1,0},{2,3},{3,2},{4,5},{5,4},{6,7},{7,6},{8,9},{9,8},{10,11... | collective-permute-start | bytes 393224 | tf_op jit(solution)/shard_map/ppermute | solution.py:251
  91.4 26.7 %collective-permute-start.3 = (bf16[2,1,128,128]{3,2,1,0:T(8,128)(2,1)S(1)}, bf16[2,1,128,128]{3,2,1,0:T(8,128)(2,1)S(1)}, u32[]{:S(2)}, u32[]{:S(2)}) collective-permute-start(bf16[2,1,128,128]{3,2,1,0:T(8,128)(2,1)S(1)} %convert_element_type.8), channel_id=1, source_target_pairs={{1,2},{3,4},{5,6},{7,8},{9,10},{11,12},{13,14},{15,16},{17,18},{19... | collective-permute-start | bytes 196616 | tf_op jit(solution)/shard_map/ppermute | solution.py:243
  118.0 1.5 %collective-permute-start.5 = (f32[2,1,128,128]{3,2,1,0:T(8,128)S(1)}, f32[2,1,128,128]{3,2,1,0:T(8,128)S(1)}, u32[]{:S(2)}, u32[]{:S(2)}) collective-permute-start(f32[2,1,128,128]{3,2,1,0:T(8,128)S(1)} %along_second_back.3), channel_id=1, source_target_pairs={{0,1},{1,0},{2,3},{3,2},{4,5},{5,4},{6,7},{7,6},{8,9},{9,8},{10,11... | collective-permute-start | bytes 393224 | tf_op jit(solution)/shard_map/ppermute | solution.py:268

commit v4 on v3

--- a/solution.py
+++ b/solution.py
@@ -47,7 +47,11 @@
     return jnp.dot(a, b, preferred_element_type=jnp.float32)
 
 
-def coil_image_kernel(core_ref, image_ref, sensitivity_ref, own_ref, other_ref):
+def opening_kernel(out_ref):
+    out_ref[...] = jnp.zeros_like(out_ref)
+
+
+def coil_image_kernel(core_ref, _, image_ref, sensitivity_ref, own_ref, other_ref):
     core = core_ref[0]
     coils = own_ref.shape[0]
     image_real, image_imaginary = image_ref[0, 0], image_ref[1, 0]
@@ -199,10 +203,11 @@
     back_third_table = held(stacked(*factor(width, grid_third, grid_third, 1.0)).T)
 
     partner_points = lax.ppermute(kernel, "core", swap)
+    opened = call(opening_kernel, "opening", shape((8, 128), f32), (), (), flops=2**30)
     own_coils, other_coils = call(
         coil_image_kernel, "coil_images",
         (shape((coils, 2 * rows_second, width), bf16),) * 2,
-        (SMEM, VMEM, VMEM), (where, image, sensitivity),
+        (SMEM, VMEM, VMEM, VMEM), (where, opened, image, sensitivity),
         flops=2**20,
     )
     partner_coils = lax.ppermute(other_coils, "core", swap)

time: 121 us -> 119 us (0.983)
  waiting for transfers between devices: 49.4 us -> 48.1 us
    all_to_all x1, waiting for transfers between devices: 24.5 us -> 22.6 us  [local(): lax.all_to_all(payload, 'chip', split_axis=0, concat_axis=0, tiled=True)]
    unnamed x18 -> x14, local copies, waits for them, and re-layouts: 3.9 us -> 2.29 us
    pallas_call x6 -> x7, Pallas kernels: 24.5 us -> 24.5 us  [call(): pl.pallas_call(kernel, name=name, out_shape=out, in_specs=[pl.BlockSpec(m...]
  transfers between devices with their start and end apart: 8 -> 8, of which waited for: 4 -> 4; matrix products, arithmetic and copies ran while one was open for 1% -> 3% of each run, Pallas kernels for 1% -> 1%
where the time goes in v4:
time: 119 us
  waiting for transfers between devices  48.1 us (40%)
  starting transfers between devices  40.3 us (34%)
  Pallas kernels  24.5 us (21%)
  local copies, waits for them, and re-layouts  3.96 us (3%)
  other arithmetic  1.99 us (2%)
    pallas_call x7, Pallas kernels, call(): pl.pallas_call(kernel, name=name, out_shape=out, in_specs=[pl.BlockSpec(m...  24.5 us
    all_to_all x1, waiting for transfers between devices, local(): lax.all_to_all(returned.reshape(groups, 2, coils, rows, width), 'chip', s...  24.4 us
    all_to_all x1, waiting for transfers between devices, local(): lax.all_to_all(payload, 'chip', split_axis=0, concat_axis=0, tiled=True)  22.6 us
    ppermute x1, starting transfers between devices, local(): partner_points = lax.ppermute(kernel, 'core', swap)  20.4 us
    all_to_all x1, starting transfers between devices, local(): lax.all_to_all(payload, 'chip', split_axis=0, concat_axis=0, tiled=True)  9.79 us
    all_to_all x1, starting transfers between devices, local(): lax.all_to_all(returned.reshape(groups, 2, coils, rows, width), 'chip', s...  7.12 us
  transfers between devices with their start and end apart: 8, of which 4 were waited for; matrix products, arithmetic and copies ran while one was open for 3% of the time, Pallas kernels for 1%

profile of v4, /device:TPU:33, one launch (start us, length us, event | category | flops | bytes accessed | tf_op | source)
XLA Modules:
  0.0 119.1 jit_solution(14291299874762545153)
XLA Ops:
  0.0 20.4 %collective-permute-start.1 = (f32[256,2,256]{2,1,0:T(2,128)}, f32[256,2,256]{2,1,0:T(2,128)S(1)}, u32[]{:S(2)}, u32[]{:S(2)}) collective-permute-start(f32[256,2,256]{2,1,0:T(2,128)} %param.11), channel_id=1, source_target_pairs={{0,1},{1,0},{2,3},{3,2},{4,5},{5,4},{6,7},{7,6},{8,9},{9,8},{10,11... | collective-permute-start | bytes 1572872 | tf_op jit(solution)/shard_map/ppermute | solution.py:205
  20.4 1.0 copy-done
  21.4 0.0 copy-done.1
  21.4 0.1 coil_images.1
  21.6 0.1 collective-permute-start
  21.7 0.7 copy-done.3
  22.4 0.4 along_second.2.own_ref
  22.8 0.4 collective-permute-done.coils_ref
  23.2 0.0 collective-permute-done.1
  23.2 19.1 %along_second.3 = bf16[64,2,3,8,128]{4,3,2,1,0:T(8,128)(2,1)} custom-call(s32[1]{0:T(128)} %bitcast.core_ref, bf16[512,256]{1,0:T(8,128)(2,1)S(1)} %copy-done.3, bf16[3,256,128]{2,1,0:T(8,128)(2,1)S(1)} %collective-permute-done.coils_ref, bf16[3,64,8,128]{3,2,1,0:T(8,128)(2,1)S(1)} %along_second.2.own_ref), custom_call_target="tpu_custom_call" | custom-call | flops 268435456 | bytes 1048576 | tf_op jit(solution)/shard_map/along_second/pallas_call | solution.py:174
  42.3 9.8 %all-to-all-start = ((bf16[64,2,3,8,128]{4,3,2,1,0:T(8,128)(2,1)}), bf16[64,2,3,8,128]{4,3,2,1,0:T(8,128)(2,1)S(1)}, u32[]{:S(2)}, u32[]{:S(2)}) async-start(bf16[64,2,3,8,128]{4,3,2,1,0:T(8,128)(2,1)} %along_second.3), calls=%async_computation | async-start | bytes 1572864 | tf_op jit(solution)/shard_map/all_to_all | solution.py:230
  52.1 0.0 copy-start.6
  52.1 0.4 stack.10
  52.5 0.6 copy-done.6
  53.1 1.2 %stack.9 = f32[1,256,512]{2,1,0:T(8,128)} reshape(f32[256,2,256]{2,1,0:T(2,128)S(1)} %copy-done.6) | data formatting | bytes 1048576 | tf_op jit(solution)/shard_map/stack | solution.py:229
  54.4 1.2 pad_maximum_fusion.points_ref
  55.5 22.6 %all-to-all-done = bf16[64,2,3,8,128]{4,3,2,1,0:T(8,128)(2,1)S(1)} async-done(((bf16[64,2,3,8,128]{4,3,2,1,0:T(8,128)(2,1)}), bf16[64,2,3,8,128]{4,3,2,1,0:T(8,128)(2,1)S(1)}, u32[]{:S(2)}, u32[]{:S(2)}) %all-to-all-start) | async-done | bytes 786464 | tf_op jit(solution)/shard_map/all_to_all | solution.py:230
  78.1 4.1 %middle.1 = bf16[128,3,8,128]{3,2,1,0:T(8,128)(2,1)} custom-call(s32[1]{0:T(128)} %bitcast.core_ref, bf16[128,3,8,128]{3,2,1,0:T(8,128)(2,1)S(1)} %bitcast.3, f32[2,256,512]{2,1,0:T(8,128)S(1)} %pad_maximum_fusion.points_ref, bf16[256,512]{1,0:T(8,128)(2,1)S(1)} %copy-done.4, bf16[512,256]{1,0:T(8,128)(2,1)S(1)} %copy-done.5, ...), custom_call_target="tpu_custom_call" | custom-call | flops 2147483648 | bytes 1048576 | tf_op jit(solution)/shard_map/middle/pallas_call | solution.py:174
  82.3 7.1 %all-to-all-start.1 = ((bf16[64,2,3,8,128]{4,3,2,1,0:T(8,128)(2,1)}), bf16[64,2,3,8,128]{4,3,2,1,0:T(8,128)(2,1)S(1)}, u32[]{:S(2)}, u32[]{:S(2)}) async-start(bf16[64,2,3,8,128]{4,3,2,1,0:T(8,128)(2,1)} %bitcast.2), calls=%async_computation.1 | async-start | bytes 1572864 | tf_op jit(solution)/shard_map/all_to_all | solution.py:243
  89.4 0.0 copy-start.2
  89.4 0.1 collective-permute-start.4
  89.6 0.5 collective-permute-start.2
  90.1 2.1 %collective-permute-start.3 = (bf16[2,1,128,128]{3,2,1,0:T(8,128)(2,1)S(1)}, bf16[2,1,128,128]{3,2,1,0:T(8,128)(2,1)S(1)}, u32[]{:S(2)}, u32[]{:S(2)}) collective-permute-start(bf16[2,1,128,128]{3,2,1,0:T(8,128)(2,1)S(1)} %convert_element_type.8), channel_id=1, source_target_pairs={{1,2},{3,4},{5,6},{7,8},{9,10},{11,12},{13,14},{15,16},{17,18},{19... | collective-permute-start | bytes 196616 | tf_op jit(solution)/shard_map/ppermute | solution.py:248
  92.2 0.0 collective-permute-done.4.sensitivity_ref
  92.2 24.4 %all-to-all-done.1.in_ref = bf16[64,2,3,8,128]{4,3,2,1,0:T(8,128)(2,1)S(1)} async-done(((bf16[64,2,3,8,128]{4,3,2,1,0:T(8,128)(2,1)}), bf16[64,2,3,8,128]{4,3,2,1,0:T(8,128)(2,1)S(1)}, u32[]{:S(2)}, u32[]{:S(2)}) %all-to-all-start.1) | async-done | bytes 786464 | tf_op jit(solution)/shard_map/all_to_all | solution.py:243
  116.6 0.4 along_second_back.3
  117.0 0.1 collective-permute-start.5
  117.1 0.0 collective-permute-done.2
  117.1 0.1 fusion.5.refs_0_
  117.3 0.4 along_second_back.2
  117.7 0.8 collective-permute-done.5
  118.4 0.7 add.29
  (12 shorter events, 0.0 us)
Async XLA Ops:
  0.0 23.2 %collective-permute-start.1 = (f32[256,2,256]{2,1,0:T(2,128)}, f32[256,2,256]{2,1,0:T(2,128)S(1)}, u32[]{:S(2)}, u32[]{:S(2)}) collective-permute-start(f32[256,2,256]{2,1,0:T(2,128)} %param.11), channel_id=1, source_target_pairs={{0,1},{1,0},{2,3},{3,2},{4,5},{5,4},{6,7},{7,6},{8,9},{9,8},{10,11... | collective-permute-start | bytes 1572872 | tf_op jit(solution)/shard_map/ppermute | solution.py:205
  20.4 1.0 copy-start
  20.4 1.0 copy-start.1
  21.4 0.9 copy-start.3
  21.6 1.6 %collective-permute-start = (bf16[3,256,128]{2,1,0:T(8,128)(2,1)S(1)}, bf16[3,256,128]{2,1,0:T(8,128)(2,1)S(1)}, u32[]{:S(2)}, u32[]{:S(2)}) collective-permute-start(bf16[3,256,128]{2,1,0:T(8,128)(2,1)S(1)} %get-tuple-element.11), channel_id=1, source_target_pairs={{0,1},{1,0},{2,3},{3,2},{4,5},{5,4},{6,7},{7,6},{8,9},{9,8},{10,11... | collective-permute-start | bytes 589832 | tf_op jit(solution)/shard_map/ppermute | solution.py:213
  42.3 35.8 %all-to-all-start = ((bf16[64,2,3,8,128]{4,3,2,1,0:T(8,128)(2,1)}), bf16[64,2,3,8,128]{4,3,2,1,0:T(8,128)(2,1)S(1)}, u32[]{:S(2)}, u32[]{:S(2)}) async-start(bf16[64,2,3,8,128]{4,3,2,1,0:T(8,128)(2,1)} %along_second.3), calls=%async_computation | async-start | bytes 1572864 | tf_op jit(solution)/shard_map/all_to_all | solution.py:230
  52.1 1.0 copy-start.6
  54.4 23.8 %copy-start.4 = (bf16[256,512]{1,0:T(8,128)(2,1)S(1)}, bf16[256,512]{1,0:T(8,128)(2,1)}, u32[]{:S(2)}) copy-start(bf16[256,512]{1,0:T(8,128)(2,1)} %constant.27.clone.third_ref.back_first_ref) | copy-start | bytes 786436
  54.4 23.8 %copy-start.5 = (bf16[512,256]{1,0:T(8,128)(2,1)S(1)}, bf16[512,256]{1,0:T(8,128)(2,1)}, u32[]{:S(2)}) copy-start(bf16[512,256]{1,0:T(8,128)(2,1)} %constant.28.clone.first_ref.back_third_ref) | copy-start | bytes 786436
  82.3 34.3 %all-to-all-start.1 = ((bf16[64,2,3,8,128]{4,3,2,1,0:T(8,128)(2,1)}), bf16[64,2,3,8,128]{4,3,2,1,0:T(8,128)(2,1)S(1)}, u32[]{:S(2)}, u32[]{:S(2)}) async-start(bf16[64,2,3,8,128]{4,3,2,1,0:T(8,128)(2,1)} %bitcast.2), calls=%async_computation.1 | async-start | bytes 1572864 | tf_op jit(solution)/shard_map/all_to_all | solution.py:243
  89.4 27.2 %copy-start.2 = (bf16[256,512]{1,0:T(8,128)(2,1)S(1)}, bf16[256,512]{1,0:T(8,128)(2,1)}, u32[]{:S(2)}) copy-start(bf16[256,512]{1,0:T(8,128)(2,1)} %constant.29.clone.table_ref) | copy-start | bytes 786436
  89.4 2.8 %collective-permute-start.4 = (bf16[3,2,1,128,128]{4,3,2,1,0:T(8,128)(2,1)S(1)}, bf16[3,2,1,128,128]{4,3,2,1,0:T(8,128)(2,1)S(1)}, u32[]{:S(2)}, u32[]{:S(2)}) collective-permute-start(bf16[3,2,1,128,128]{4,3,2,1,0:T(8,128)(2,1)S(1)} %constant_dynamic-slice_fusion), channel_id=1, source_target_pairs={{0,1},{1,0},{2,3},{3,2},{4,5},{5,4},{6,7},{7,6},{8,9},{9,8},{10,11... | collective-permute-start | bytes 589832 | tf_op jit(solution)/shard_map/ppermute | solution.py:253
  89.6 27.5 %collective-permute-start.2 = (f32[2,1,128,128]{3,2,1,0:T(8,128)S(1)}, f32[2,1,128,128]{3,2,1,0:T(8,128)S(1)}, u32[]{:S(2)}, u32[]{:S(2)}) collective-permute-start(f32[2,1,128,128]{3,2,1,0:T(8,128)S(1)} %copy-done.1), channel_id=1, source_target_pairs={{0,1},{1,0},{2,3},{3,2},{4,5},{5,4},{6,7},{7,6},{8,9},{9,8},{10,11... | collective-permute-start | bytes 393224 | tf_op jit(solution)/shard_map/ppermute | solution.py:256
  90.1 27.0 %collective-permute-start.3 = (bf16[2,1,128,128]{3,2,1,0:T(8,128)(2,1)S(1)}, bf16[2,1,128,128]{3,2,1,0:T(8,128)(2,1)S(1)}, u32[]{:S(2)}, u32[]{:S(2)}) collective-permute-start(bf16[2,1,128,128]{3,2,1,0:T(8,128)(2,1)S(1)} %convert_element_type.8), channel_id=1, source_target_pairs={{1,2},{3,4},{5,6},{7,8},{9,10},{11,12},{13,14},{15,16},{17,18},{19... | collective-permute-start | bytes 196616 | tf_op jit(solution)/shard_map/ppermute | solution.py:248
  117.0 1.5 %collective-permute-start.5 = (f32[2,1,128,128]{3,2,1,0:T(8,128)S(1)}, f32[2,1,128,128]{3,2,1,0:T(8,128)S(1)}, u32[]{:S(2)}, u32[]{:S(2)}) collective-permute-start(f32[2,1,128,128]{3,2,1,0:T(8,128)S(1)} %along_second_back.3), channel_id=1, source_target_pairs={{0,1},{1,0},{2,3},{3,2},{4,5},{5,4},{6,7},{7,6},{8,9},{9,8},{10,11... | collective-permute-start | bytes 393224 | tf_op jit(solution)/shard_map/ppermute | solution.py:273

commit v5 on v4

--- a/solution.py
+++ b/solution.py
@@ -98,12 +98,11 @@
 
 
 def middle_kernel(
-    core_ref, in_ref, points_ref, third_ref, first_ref, back_first_ref, back_third_ref,
+    in_ref, points_ref, third_ref, first_ref, back_first_ref, back_third_ref,
     out_ref, lines, both, spread, filtered, back, built, left,
 ):
     count, coils, rows, width = in_ref.shape
     grid = points_ref.shape[1]
-    core = core_ref[0]
     frequencies = rows // 2
     part_of = [slice(j * count, (j + 1) * count) for j in range(frequencies)]
 
@@ -123,7 +122,7 @@
             spread[j, :count] = third[:, :grid]
             spread[j, count:] = third[:, grid:]
         for j in range(frequencies):
-            place = core if j < frequencies // 2 else 1 - core
+            place = j // (frequencies // 2)
             at = j % (frequencies // 2) * grid
             for part in range(2):
                 half = slice(part * grid, (part + 1) * grid)
@@ -226,13 +225,15 @@
         (VMEM((coils, groups, rows, width), bf16), copies((2, coils))),
         flops=2**28, to=HBM,
     )
-    points = jnp.stack([own_points, partner_points]).reshape(2, grid, pair * grid_third)
+    first_points = jnp.where(core == 0, own_points, partner_points)
+    second_points = jnp.where(core == 0, partner_points, own_points)
+    points = jnp.stack([first_points, second_points]).reshape(2, grid, pair * grid_third)
     received = lax.all_to_all(payload, "chip", split_axis=0, concat_axis=0, tiled=True)
     returned = call(
         middle_kernel, "middle",
         shape((size, coils, rows, width), bf16),
-        (SMEM,) + (VMEM,) * 6,
-        (where, received.reshape(size, coils, rows, width), points,
+        (VMEM,) * 6,
+        (received.reshape(size, coils, rows, width), points,
          third_table, first_table, back_first_table, back_third_table),
         (VMEM((size * rows, width), f32), VMEM((2 * pair * size, 2 * width), bf16),
          VMEM((2 * pair, 2 * size, grid_third), bf16), VMEM((2 * pair, 2 * grid, grid_third), bf16),

time: 119 us -> 120 us (level)
  no operation moved by 1% of the time
where the time goes in v5:
time: 120 us; the launch traced here: 119 us
  waiting for transfers between devices  48.7 us (41%)
  starting transfers between devices  40.4 us (34%)
  Pallas kernels  24.5 us (20%)
  local copies, waits for them, and re-layouts  3.35 us (3%)
  other arithmetic  2.06 us (2%)
    pallas_call x7, Pallas kernels, call(): pl.pallas_call(kernel, name=name, out_shape=out, in_specs=[pl.BlockSpec(m...  24.5 us
    all_to_all x1, waiting for transfers between devices, local(): lax.all_to_all(returned.reshape(groups, 2, coils, rows, width), 'chip', s...  24.3 us
    all_to_all x1, waiting for transfers between devices, local(): lax.all_to_all(payload, 'chip', split_axis=0, concat_axis=0, tiled=True)  23.2 us
    ppermute x1, starting transfers between devices, local(): partner_points = lax.ppermute(kernel, 'core', swap)  20.4 us
    all_to_all x1, starting transfers between devices, local(): lax.all_to_all(payload, 'chip', split_axis=0, concat_axis=0, tiled=True)  9.92 us
    all_to_all x1, starting transfers between devices, local(): lax.all_to_all(returned.reshape(groups, 2, coils, rows, width), 'chip', s...  7.07 us
  transfers between devices with their start and end apart: 8, of which 4 were waited for; matrix products, arithmetic and copies ran while one was open for 3% of the time, Pallas kernels for 1%

profile of v5, /device:TPU:33, one launch (start us, length us, event | category | flops | bytes accessed | tf_op | source)
XLA Modules:
  0.0 119.2 jit_solution(3960049330663764618)
XLA Ops:
  0.0 20.4 %collective-permute-start.1 = (f32[256,2,256]{2,1,0:T(2,128)}, f32[256,2,256]{2,1,0:T(2,128)S(1)}, u32[]{:S(2)}, u32[]{:S(2)}) collective-permute-start(f32[256,2,256]{2,1,0:T(2,128)} %param.11), channel_id=1, source_target_pairs={{0,1},{1,0},{2,3},{3,2},{4,5},{5,4},{6,7},{7,6},{8,9},{9,8},{10,11... | collective-permute-start | bytes 1572872 | tf_op jit(solution)/shard_map/ppermute | solution.py:204
  20.4 1.0 copy-done
  21.4 0.0 copy-done.1
  21.4 0.1 coil_images.1
  21.6 0.1 collective-permute-start
  21.7 0.7 copy-done.3
  22.4 0.4 along_second.2.own_ref
  22.8 0.4 collective-permute-done.coils_ref
  23.2 0.0 collective-permute-done.1
  23.2 19.2 %along_second.3 = bf16[64,2,3,8,128]{4,3,2,1,0:T(8,128)(2,1)} custom-call(s32[1]{0:T(128)} %bitcast.core_ref, bf16[512,256]{1,0:T(8,128)(2,1)S(1)} %copy-done.3, bf16[3,256,128]{2,1,0:T(8,128)(2,1)S(1)} %collective-permute-done.coils_ref, bf16[3,64,8,128]{3,2,1,0:T(8,128)(2,1)S(1)} %along_second.2.own_ref), custom_call_target="tpu_custom_call" | custom-call | flops 268435456 | bytes 1048576 | tf_op jit(solution)/shard_map/along_second/pallas_call | solution.py:173
  42.3 0.0 copy-start.6
  42.3 9.9 %all-to-all-start = ((bf16[64,2,3,8,128]{4,3,2,1,0:T(8,128)(2,1)}), bf16[64,2,3,8,128]{4,3,2,1,0:T(8,128)(2,1)S(1)}, u32[]{:S(2)}, u32[]{:S(2)}) async-start(bf16[64,2,3,8,128]{4,3,2,1,0:T(8,128)(2,1)} %along_second.3), calls=%async_computation | async-start | bytes 1572864 | tf_op jit(solution)/shard_map/all_to_all | solution.py:231
  52.3 0.1 broadcast_select_fusion.1
  52.3 0.4 stack.10
  52.8 1.2 %stack.9 = f32[1,256,512]{2,1,0:T(8,128)} reshape(f32[256,2,256]{2,1,0:T(2,128)S(1)} %bitcast.8) | data formatting | bytes 1048576 | tf_op jit(solution)/shard_map/stack | solution.py:230
  54.0 1.2 pad_maximum_fusion.points_ref
  55.2 23.2 %all-to-all-done = bf16[64,2,3,8,128]{4,3,2,1,0:T(8,128)(2,1)S(1)} async-done(((bf16[64,2,3,8,128]{4,3,2,1,0:T(8,128)(2,1)}), bf16[64,2,3,8,128]{4,3,2,1,0:T(8,128)(2,1)S(1)}, u32[]{:S(2)}, u32[]{:S(2)}) %all-to-all-start) | async-done | bytes 786464 | tf_op jit(solution)/shard_map/all_to_all | solution.py:231
  78.4 4.1 %middle.1 = bf16[128,3,8,128]{3,2,1,0:T(8,128)(2,1)} custom-call(bf16[128,3,8,128]{3,2,1,0:T(8,128)(2,1)S(1)} %bitcast.7, f32[2,256,512]{2,1,0:T(8,128)S(1)} %pad_maximum_fusion.points_ref, bf16[256,512]{1,0:T(8,128)(2,1)S(1)} %copy-done.4, bf16[512,256]{1,0:T(8,128)(2,1)S(1)} %copy-done.5, bf16[256,512]{1,0:T(8,128)(2,1)S(1)} %copy-done.4, ...), custom_call_target="tpu_custom_call" | custom-call | flops 2147483648 | bytes 1048576 | tf_op jit(solution)/shard_map/middle/pallas_call | solution.py:173
  82.4 7.1 %all-to-all-start.1 = ((bf16[64,2,3,8,128]{4,3,2,1,0:T(8,128)(2,1)}), bf16[64,2,3,8,128]{4,3,2,1,0:T(8,128)(2,1)S(1)}, u32[]{:S(2)}, u32[]{:S(2)}) async-start(bf16[64,2,3,8,128]{4,3,2,1,0:T(8,128)(2,1)} %bitcast.2), calls=%async_computation.1 | async-start | bytes 1572864 | tf_op jit(solution)/shard_map/all_to_all | solution.py:244
  89.5 0.0 copy-start.2
  89.6 0.1 collective-permute-start.4
  89.7 0.5 collective-permute-start.2
  90.2 2.1 %collective-permute-start.3 = (bf16[2,1,128,128]{3,2,1,0:T(8,128)(2,1)S(1)}, bf16[2,1,128,128]{3,2,1,0:T(8,128)(2,1)S(1)}, u32[]{:S(2)}, u32[]{:S(2)}) collective-permute-start(bf16[2,1,128,128]{3,2,1,0:T(8,128)(2,1)S(1)} %convert_element_type.8), channel_id=1, source_target_pairs={{1,2},{3,4},{5,6},{7,8},{9,10},{11,12},{13,14},{15,16},{17,18},{19... | collective-permute-start | bytes 196616 | tf_op jit(solution)/shard_map/ppermute | solution.py:249
  92.3 0.0 collective-permute-done.4.sensitivity_ref
  92.4 24.3 %all-to-all-done.1.in_ref = bf16[64,2,3,8,128]{4,3,2,1,0:T(8,128)(2,1)S(1)} async-done(((bf16[64,2,3,8,128]{4,3,2,1,0:T(8,128)(2,1)}), bf16[64,2,3,8,128]{4,3,2,1,0:T(8,128)(2,1)S(1)}, u32[]{:S(2)}, u32[]{:S(2)}) %all-to-all-start.1) | async-done | bytes 786464 | tf_op jit(solution)/shard_map/all_to_all | solution.py:244
  116.7 0.4 along_second_back.3
  117.0 0.1 collective-permute-start.5
  117.2 0.0 collective-permute-done.3
  117.2 0.1 fusion.5.refs_0_
  117.3 0.4 along_second_back.2
  117.7 0.8 collective-permute-done.5
  118.5 0.7 add.29
  (13 shorter events, 0.1 us)
Async XLA Ops:
  0.0 23.2 %collective-permute-start.1 = (f32[256,2,256]{2,1,0:T(2,128)}, f32[256,2,256]{2,1,0:T(2,128)S(1)}, u32[]{:S(2)}, u32[]{:S(2)}) collective-permute-start(f32[256,2,256]{2,1,0:T(2,128)} %param.11), channel_id=1, source_target_pairs={{0,1},{1,0},{2,3},{3,2},{4,5},{5,4},{6,7},{7,6},{8,9},{9,8},{10,11... | collective-permute-start | bytes 1572872 | tf_op jit(solution)/shard_map/ppermute | solution.py:204
  20.4 1.0 copy-start
  20.4 1.0 copy-start.1
  21.4 0.9 copy-start.3
  21.6 1.6 %collective-permute-start = (bf16[3,256,128]{2,1,0:T(8,128)(2,1)S(1)}, bf16[3,256,128]{2,1,0:T(8,128)(2,1)S(1)}, u32[]{:S(2)}, u32[]{:S(2)}) collective-permute-start(bf16[3,256,128]{2,1,0:T(8,128)(2,1)S(1)} %get-tuple-element.11), channel_id=1, source_target_pairs={{0,1},{1,0},{2,3},{3,2},{4,5},{5,4},{6,7},{7,6},{8,9},{9,8},{10,11... | collective-permute-start | bytes 589832 | tf_op jit(solution)/shard_map/ppermute | solution.py:212
  42.3 9.9 %copy-start.6 = (f32[256,2,256]{2,1,0:T(2,128)S(1)}, f32[256,2,256]{2,1,0:T(2,128)}, u32[]{:S(2)}) copy-start(f32[256,2,256]{2,1,0:T(2,128)} %param.11) | copy-start | bytes 1572868
  42.3 36.0 %all-to-all-start = ((bf16[64,2,3,8,128]{4,3,2,1,0:T(8,128)(2,1)}), bf16[64,2,3,8,128]{4,3,2,1,0:T(8,128)(2,1)S(1)}, u32[]{:S(2)}, u32[]{:S(2)}) async-start(bf16[64,2,3,8,128]{4,3,2,1,0:T(8,128)(2,1)} %along_second.3), calls=%async_computation | async-start | bytes 1572864 | tf_op jit(solution)/shard_map/all_to_all | solution.py:231
  54.0 24.4 %copy-start.4 = (bf16[256,512]{1,0:T(8,128)(2,1)S(1)}, bf16[256,512]{1,0:T(8,128)(2,1)}, u32[]{:S(2)}) copy-start(bf16[256,512]{1,0:T(8,128)(2,1)} %constant.27.clone.third_ref.back_first_ref) | copy-start | bytes 786436
  54.0 24.4 %copy-start.5 = (bf16[512,256]{1,0:T(8,128)(2,1)S(1)}, bf16[512,256]{1,0:T(8,128)(2,1)}, u32[]{:S(2)}) copy-start(bf16[512,256]{1,0:T(8,128)(2,1)} %constant.28.clone.first_ref.back_third_ref) | copy-start | bytes 786436
  82.4 34.2 %all-to-all-start.1 = ((bf16[64,2,3,8,128]{4,3,2,1,0:T(8,128)(2,1)}), bf16[64,2,3,8,128]{4,3,2,1,0:T(8,128)(2,1)S(1)}, u32[]{:S(2)}, u32[]{:S(2)}) async-start(bf16[64,2,3,8,128]{4,3,2,1,0:T(8,128)(2,1)} %bitcast.2), calls=%async_computation.1 | async-start | bytes 1572864 | tf_op jit(solution)/shard_map/all_to_all | solution.py:244
  89.5 27.1 %copy-start.2 = (bf16[256,512]{1,0:T(8,128)(2,1)S(1)}, bf16[256,512]{1,0:T(8,128)(2,1)}, u32[]{:S(2)}) copy-start(bf16[256,512]{1,0:T(8,128)(2,1)} %constant.29.clone.table_ref) | copy-start | bytes 786436
  89.6 2.8 %collective-permute-start.4 = (bf16[3,2,1,128,128]{4,3,2,1,0:T(8,128)(2,1)S(1)}, bf16[3,2,1,128,128]{4,3,2,1,0:T(8,128)(2,1)S(1)}, u32[]{:S(2)}, u32[]{:S(2)}) collective-permute-start(bf16[3,2,1,128,128]{4,3,2,1,0:T(8,128)(2,1)S(1)} %constant_dynamic-slice_fusion), channel_id=1, source_target_pairs={{0,1},{1,0},{2,3},{3,2},{4,5},{5,4},{6,7},{7,6},{8,9},{9,8},{10,11... | collective-permute-start | bytes 589832 | tf_op jit(solution)/shard_map/ppermute | solution.py:254
  89.7 27.5 %collective-permute-start.2 = (f32[2,1,128,128]{3,2,1,0:T(8,128)S(1)}, f32[2,1,128,128]{3,2,1,0:T(8,128)S(1)}, u32[]{:S(2)}, u32[]{:S(2)}) collective-permute-start(f32[2,1,128,128]{3,2,1,0:T(8,128)S(1)} %copy-done.1), channel_id=1, source_target_pairs={{0,1},{1,0},{2,3},{3,2},{4,5},{5,4},{6,7},{7,6},{8,9},{9,8},{10,11... | collective-permute-start | bytes 393224 | tf_op jit(solution)/shard_map/ppermute | solution.py:257
  90.2 27.0 %collective-permute-start.3 = (bf16[2,1,128,128]{3,2,1,0:T(8,128)(2,1)S(1)}, bf16[2,1,128,128]{3,2,1,0:T(8,128)(2,1)S(1)}, u32[]{:S(2)}, u32[]{:S(2)}) collective-permute-start(bf16[2,1,128,128]{3,2,1,0:T(8,128)(2,1)S(1)} %convert_element_type.8), channel_id=1, source_target_pairs={{1,2},{3,4},{5,6},{7,8},{9,10},{11,12},{13,14},{15,16},{17,18},{19... | collective-permute-start | bytes 196616 | tf_op jit(solution)/shard_map/ppermute | solution.py:249
  117.0 1.5 %collective-permute-start.5 = (f32[2,1,128,128]{3,2,1,0:T(8,128)S(1)}, f32[2,1,128,128]{3,2,1,0:T(8,128)S(1)}, u32[]{:S(2)}, u32[]{:S(2)}) collective-permute-start(f32[2,1,128,128]{3,2,1,0:T(8,128)S(1)} %along_second_back.3), channel_id=1, source_target_pairs={{0,1},{1,0},{2,3},{3,2},{4,5},{5,4},{6,7},{7,6},{8,9},{9,8},{10,11... | collective-permute-start | bytes 393224 | tf_op jit(solution)/shard_map/ppermute | solution.py:274
